TPU v7x, 32 devices: a whole 2x2x4 slice. The times are simulated.
32 devices in a mesh: sub: 8 (over z, y), slab: 4 (over x, core).
Axes of the slice: x: 2, y: 2, z: 4, core: 2. Of those that a mesh axis runs over, the one named last changes fastest.
Arguments:
- rhs: float32 [8, 64, 8, 512], P(None, 'sub', None, 'slab'), may hold values from -60 to 60, as said below
- perm: float32 [64, 8, 512], P('sub', None, 'slab'), may hold values from 0.1 to 10
- accum: float32 [64, 8, 512], P('sub', None, 'slab'), may hold values from 0.05 to 0.5
- counts: int32 [8], replicated, may hold values from 1 to 8, as said below
Outputs:
- solution: float32 [8, 64, 8, 512], P(None, 'sub', None, 'slab')
- residual: float32 [8, 64, 8, 512], P(None, 'sub', None, 'slab')
Inputs may be any that keep to these rules, and one draw needn't show every extreme that they name: `rhs`: pressure sources of the 8 systems; values on planes that are not live are never read. counts[i] live planes fill the first slots of subdomain i; some subdomain has 8.
All inputs are finite; a program needn't handle non-finite values.
Results may differ from a plain program's by a relative error of at most 0.00045.
Values sent between devices are 32-bit elements; how exact they have to be, the bound alone decides.
A program may use at most 64 MiB of HBM per device.

v0:
```python
import functools

import jax
import jax.numpy as jnp
from jax import lax
from jax.experimental import pallas as pl
from jax.experimental.pallas import tpu as pltpu
from jax.sharding import PartitionSpec as P

S = 8
ITERS = 4
DEG = 4


cheb_low = 0.05
cheb_high = 2.0


def with_halo(cells, sides, width):
    for axis, dim in sides:
        count = lax.axis_size(axis)
        ends = count - 1
        head = lax.slice_in_dim(cells, 0, width, axis=dim)
        tail = lax.slice_in_dim(cells, cells.shape[dim] - width, cells.shape[dim], axis=dim)
        cells = jnp.concatenate(
            [
                lax.ppermute(tail, axis, [(i, (i + 1) % count) for i in range(ends)]),
                cells,
                lax.ppermute(head, axis, [((i + 1) % count, i) for i in range(ends)]),
            ],
            axis=dim,
        )
    return cells


def neighbours(field, live, plane):
    first = field[:, 0]
    last = lax.dynamic_index_in_dim(field, live - 1, 1, keepdims=False)
    edges = with_halo(jnp.stack([first, last], axis=1), (("sub", 1),), 1)
    before = edges[:, 0:1]
    after = edges[:, 3:4]
    zero_plane = jnp.zeros_like(field[:, :1])
    up_inside = jnp.concatenate([field[:, 1:], zero_plane], axis=1)
    down_inside = jnp.concatenate([zero_plane, field[:, :-1]], axis=1)
    x_next = jnp.where(plane == live - 1, after, up_inside)
    x_prev = jnp.where(plane == 0, before, down_inside)
    zero_row = jnp.zeros_like(field[:, :, :1])
    y_next = jnp.concatenate([field[:, :, 1:], zero_row], axis=2)
    y_prev = jnp.concatenate([zero_row, field[:, :, :-1]], axis=2)
    padded = with_halo(field, (("slab", 3),), 1)
    z_next = padded[..., 2:]
    z_prev = padded[..., :-2]
    return (x_next, x_prev, y_next, y_prev, z_next, z_prev)


def product(left, right):
    return lax.dot_general(
        left.reshape(left.shape[0], -1),
        right.reshape(right.shape[0], -1),
        (((1,), (1,)), ((), ())),
        precision=lax.Precision.HIGHEST,
    )


def combine(coef, block):
    flat = jnp.dot(coef, block.reshape(block.shape[0], -1), precision=lax.Precision.HIGHEST)
    return flat.reshape(block.shape)


def lower_solve(factor, block):
    flat = jax.scipy.linalg.solve_triangular(factor, block.reshape(block.shape[0], -1), lower=True)
    return flat.reshape(block.shape)


def precondition(vector, operate, inv_diag):
    theta = 0.5 * (cheb_high + cheb_low)
    delta = 0.5 * (cheb_high - cheb_low)
    sigma = theta / delta
    remain = vector
    update = inv_diag * remain * (1.0 / theta)
    result = update
    rho = 1.0 / sigma
    for step in range(DEG - 1):
        remain = remain - operate(update)
        rho_next = 1.0 / (2.0 * sigma - rho)
        update = rho_next * rho * update + 2.0 * rho_next / delta * (inv_diag * remain)
        result = result + update
        rho = rho_next
    return result


def small_solve(coefs, lowers, lead):
    hess = jnp.zeros((ITERS * S, (ITERS + 1) * S), jnp.float32)
    for j in range(ITERS):
        for i in range(j + 1):
            hess = hess.at[j * S : (j + 1) * S, i * S : (i + 1) * S].set(coefs[j][i])
        hess = hess.at[j * S : (j + 1) * S, (j + 1) * S : (j + 2) * S].set(lowers[j])
    target = jnp.zeros((S, (ITERS + 1) * S), jnp.float32).at[:, :S].set(lead)
    normal = jnp.dot(hess, hess.T, precision=lax.Precision.HIGHEST)
    right = jnp.dot(hess, target.T, precision=lax.Precision.HIGHEST)
    factor = jnp.linalg.cholesky(normal)
    mix = jax.scipy.linalg.cho_solve((factor, True), right).T
    return (mix, hess, target)


def body(rhs, perm, accum, counts):
    live = counts[lax.axis_index("sub")]
    depth = rhs.shape[1]
    plane = lax.broadcasted_iota(jnp.int32, (1, depth, 1, 1), 1)
    mask = (plane < live).astype(jnp.float32)
    field_perm = perm[None]
    near = neighbours(field_perm, live, plane)
    conduct = []
    diag = accum[None]
    for other in near:
        weight = 2.0 * field_perm * other / (field_perm + other)
        conduct.append(weight)
        diag = diag + weight
    inv_diag = mask / diag

    def operate(field):
        beside = neighbours(field, live, plane)
        total = diag * field
        for weight, other in zip(conduct, beside):
            total = total - weight * other
        return mask * total

    start = rhs * mask
    lead = jnp.linalg.cholesky(lax.psum(product(start, start), ("sub", "slab")))
    basis = [lower_solve(lead, start)]
    coefs = []
    lowers = []
    for step in range(ITERS):
        direction = precondition(basis[step], operate, inv_diag)
        work = operate(direction)
        stacked, whole = lax.psum(
            (jnp.stack([product(work, basis[i]) for i in range(step + 1)]), product(work, work)),
            ("sub", "slab"),
        )
        found = [stacked[i] for i in range(step + 1)]
        block = whole
        for i in range(step + 1):
            work = work - combine(found[i], basis[i])
            block = block - jnp.dot(found[i], found[i].T, precision=lax.Precision.HIGHEST)
        lower = jnp.linalg.cholesky(block)
        basis.append(lower_solve(lower, work))
        coefs.append(found)
        lowers.append(lower)
    mix, hess, target = small_solve(coefs, lowers, lead)
    combo = combine(mix[:, :S], basis[0])
    for j in range(1, ITERS):
        combo = combo + combine(mix[:, j * S : (j + 1) * S], basis[j])
    solution = precondition(combo, operate, inv_diag)
    residual = start - operate(solution)
    return (solution, residual)

LANES = 128


def full(dims, left, right):
    return lax.dot_general(
        left,
        right,
        (dims, ((), ())),
        precision=lax.Precision.HIGHEST,
        preferred_element_type=jnp.float32,
    )


def chebyshev_steps():
    theta = 0.5 * (cheb_high + cheb_low)
    delta = 0.5 * (cheb_high - cheb_low)
    sigma = theta / delta
    rho = 1.0 / sigma
    steps = []
    for _ in range(DEG - 1):
        rho_next = 1.0 / (2.0 * sigma - rho)
        steps.append((rho_next * rho, 2.0 * rho_next / delta))
        rho = rho_next
    return 1.0 / theta, steps


def eliminate(mat, rows, jordan):
    row = lax.broadcasted_iota(jnp.int32, mat.shape, 0)
    for k in range(rows):
        column = jnp.broadcast_to(mat[:, k : k + 1], mat.shape)
        pivot = column[k : k + 1, :]
        line = mat[k : k + 1, :]
        if jordan:
            scaled = line / pivot
            mat = jnp.where(row == k, scaled, mat - column * scaled)
        else:
            root = lax.rsqrt(pivot)
            root = root * (1.5 - 0.5 * pivot * root * root)
            scaled = line * root
            mat = jnp.where(row == k, scaled, jnp.where(row > k, mat - column * root * scaled, mat))
    return mat


def kernel(
    dims,
    rhs_ref, perm_ref, accum_ref, counts_ref, out0_ref, out1_ref,
    pick_ref, raw_ref, out_ref, in_buf, in_got, out_buf, out_got,
    ext, coef, big, near_lo, near_hi, d0, d1, rem, sol, start_own,
    part, got1, mid, got2, tmp, hess, normal,
    in_send, in_recv, out_send, out_recv, xs_send, xs_recv, halo_send, halo_recv, s1_send, s1_recv, s2_send, s2_recv,
):
    nsub, nslab, zl, yl_n, pack, nx = dims
    halo = DEG
    pad = halo + 1
    span = zl + 2 * halo
    per = yl_n + 1
    sub = lax.axis_index("sub")
    slab = lax.axis_index("slab")

    def position(i):
        across = lax.rem(i, 2)
        at = i // 2 + across * (nsub - 1 - 2 * (i // 2))
        return at + lax.rem(slab, 2) * (nsub - 1 - 2 * at)

    place = slab * nsub + position(sub)
    total = nsub * nslab
    nxt = lax.rem(place + 1, total)
    prv = lax.rem(place + total - 1, total)

    def dev(g):
        at = lax.rem(g, nsub)
        at = at + lax.rem(g // nsub, 2) * (nsub - 1 - 2 * at)
        across = at // (nsub // 2)
        return {"sub": 2 * (at + across * (nsub - 1 - 2 * at)) + across, "slab": g // nsub}

    barrier = pltpu.get_barrier_semaphore()
    for d in range(1, nslab):
        pl.semaphore_signal(
            barrier, inc=1, device_id={"slab": lax.rem(slab + d, nslab)}, device_id_type=pl.DeviceIdType.MESH
        )
    for d in range(1, nsub):
        pl.semaphore_signal(
            barrier, inc=1, device_id={"sub": lax.rem(sub + d, nsub)}, device_id_type=pl.DeviceIdType.MESH
        )
    for g in (nxt, prv):
        pl.semaphore_signal(barrier, inc=1, device_id=dev(g), device_id_type=pl.DeviceIdType.MESH)

    def remote(src, dst, send, recv, device):
        return pltpu.make_async_remote_copy(
            src_ref=src, dst_ref=dst, send_sem=send, recv_sem=recv,
            device_id=device, device_id_type=pl.DeviceIdType.MESH,
        )

    group = pack * (LANES // (pack * nsub))
    wide_row = lax.broadcasted_iota(jnp.int32, (LANES, LANES), 0)
    wide_lane = lax.broadcasted_iota(jnp.int32, (LANES, LANES), 1)
    rank = lax.rem(wide_row, group) // pack
    owner = wide_row // group
    base_of = jnp.zeros_like(wide_row)
    live_of = jnp.zeros_like(wide_row)
    before = jnp.int32(0)
    for i in range(nsub):
        live = counts_ref[i]
        base_of = jnp.where(owner == i, before, base_of)
        live_of = jnp.where(owner == i, live, live_of)
        before = before + live
    goal = base_of + rank + lax.rem(wide_row, pack) * nx
    pick_ref[...] = jnp.where((rank < live_of) & (goal == wide_lane), 1.0, 0.0).astype(jnp.float32)

    for y in range(yl_n):
        in_buf[y] = rhs_ref[pl.ds(y, LANES, stride=yl_n), :].T
    pieces = [ref[pl.ds(y, group, stride=yl_n), :] for ref in (perm_ref, accum_ref) for y in range(yl_n)]
    in_buf[yl_n] = jnp.concatenate(pieces, axis=0).T

    pl.semaphore_wait(barrier, nslab + nsub)

    def rows_of(i):
        return pl.ds(pl.multiple_of(position(i) * zl, 8), zl)

    arrivals = []
    for d in range(1, nsub):
        peer = lax.rem(sub + d, nsub)
        c = remote(in_buf.at[:, rows_of(peer), :], in_got.at[sub], in_send.at[d], in_recv.at[sub], {"sub": peer})
        c.start()
        arrivals.append(c)
    in_got[sub] = in_buf[:, rows_of(sub), :]
    for d in range(1, nsub):
        peer = lax.rem(sub + d, nsub)
        remote(in_buf.at[:, rows_of(peer), :], in_got.at[peer], in_send.at[d], in_recv.at[peer], {"sub": peer}).wait_recv()

    strip = lax.broadcasted_iota(jnp.int32, (zl, LANES), 1) // group

    def butterfly(items):
        d = len(items) // 2
        while d:
            fresh = list(items)
            for a in range(len(items)):
                if a & d:
                    continue
                first_half = (strip & d) == 0
                fresh[a] = jnp.where(first_half, items[a], pltpu.roll(items[a + d], group * d, 1))
                fresh[a + d] = jnp.where(first_half, pltpu.roll(items[a], LANES - group * d, 1), items[a + d])
            items = fresh
            d //= 2
        return items

    for t in range(per):
        for i, value in enumerate(butterfly([in_got[i, t] for i in range(nsub)])):
            raw_ref[pl.ds(t * 8 + i, zl, stride=per * 8), :] = value

    packed = full(((1,), (0,)), raw_ref[...], pick_ref[...])
    for k in range(zl * per):
        at = (pad * per + k) * LANES
        ext[:, at : at + LANES] = packed[k * 8 : k * 8 + 8, :]
    edge = pad * per * LANES
    whole = zl * per * LANES
    up = remote(ext.at[:, whole : whole + edge], ext.at[:, 0:edge], xs_send.at[0], xs_recv.at[0], dev(nxt))
    down = remote(ext.at[:, edge : 2 * edge], ext.at[:, edge + whole : 2 * edge + whole], xs_send.at[1], xs_recv.at[1], dev(prv))
    up.start()
    down.start()

    lane = lax.broadcasted_iota(jnp.int32, (8, LANES), 1)
    row = lax.broadcasted_iota(jnp.int32, (8, LANES), 0)
    tile = yl_n * LANES
    own_lo, own_hi = halo * tile, (halo + zl) * tile

    for k in range(zl):
        a = (pad + k) * per * LANES
        start_own[:, k * tile : (k + 1) * tile] = ext[:, a : a + tile]
        big[0:8, (halo + k) * tile : (halo + k + 1) * tile] = ext[:, a : a + tile]

    def products(blocks):
        def add(k, accs):
            accs = list(accs)
            for h in range(2):
                at = pl.ds(pl.multiple_of((2 * k + h) * LANES + own_lo, LANES), LANES)
                w = big[0:8, at]
                turned = [w] + [pltpu.roll(w, n, 0) for n in range(1, 8)]
                for b in range(blocks):
                    v = w if b == 0 else big[8 * b : 8 * b + 8, at]
                    for n in range(8):
                        accs[8 * b + n] = accs[8 * b + n] + v * turned[n]
            return tuple(accs)

        zero = jnp.zeros((8, LANES), jnp.float32)
        accs = lax.fori_loop(0, zl * yl_n // 2, add, (zero,) * (8 * blocks))
        out = zero
        for b in range(blocks):
            for n in range(8):
                acc = accs[8 * b + n]
                acc = pltpu.roll(acc, 8 - n, 0) if n else acc
                line = jnp.sum(acc, axis=1, keepdims=True)
                out = jnp.where(lane == 8 * b + lax.rem(row + n, 8), line, out)
        return out

    def reduce_begin(r, gram):
        part[r] = gram
        got1[r, slab] = part[r]
        copies = []
        for d in range(1, nslab):
            peer = lax.rem(slab + d, nslab)
            c = remote(part.at[r], got1.at[r, slab], s1_send.at[r, d], s1_recv.at[r, slab], {"slab": peer})
            c.start()
            copies.append(c)
        return copies

    def reduce_end(r, copies):
        for d in range(1, nslab):
            peer = lax.rem(slab + d, nslab)
            remote(part.at[r], got1.at[r, peer], s1_send.at[r, d], s1_recv.at[r, peer], {"slab": peer}).wait_recv()
        acc = got1[r, 0]
        for i in range(1, nslab):
            acc = acc + got1[r, i]
        mid[r] = acc
        got2[r, sub] = acc
        for d in range(1, nsub):
            peer = lax.rem(sub + d, nsub)
            c = remote(mid.at[r], got2.at[r, sub], s2_send.at[r, d], s2_recv.at[r, sub], {"sub": peer})
            c.start()
            copies.append(c)
        for d in range(1, nsub):
            peer = lax.rem(sub + d, nsub)
            remote(mid.at[r], got2.at[r, peer], s2_send.at[r, d], s2_recv.at[r, peer], {"sub": peer}).wait_recv()
        acc = got2[r, 0]
        for i in range(1, nsub):
            acc = acc + got2[r, i]
        for c in copies:
            c.wait_send()
        return acc

    begun = reduce_begin(0, products(1))

    up.wait()
    down.wait()
    low = jnp.where(place == 0, 0.0, 1.0).astype(jnp.float32)
    high = jnp.where(place == total - 1, 0.0, 1.0).astype(jnp.float32)
    for k in range(pad):
        a = (k * per + yl_n) * LANES
        ext[:, a : a + LANES] = ext[:, a : a + LANES] * low
        b = ((pad + zl + k) * per + yl_n) * LANES
        ext[:, b : b + LANES] = ext[:, b : b + LANES] * high
    along = lax.rem(lane, nx)

    def fill(e, _):
        def grab(t):
            return ext[:, pl.ds(pl.multiple_of(((e + 1 + t) * per + yl_n) * LANES, LANES), LANES)]

        here, after, before = grab(0), grab(1), grab(-1)
        swap_up = pltpu.roll(here, LANES - nx, 1)
        swap_down = pltpu.roll(here, nx, 1)
        x_up = jnp.where(along == nx - 1, 0.0, pltpu.roll(here, LANES - 1, 1))
        x_down = jnp.where(along == 0, 0.0, pltpu.roll(here, 1, 1))
        swap_up = jnp.where(lane >= LANES - nx, 0.0, swap_up)
        swap_down = jnp.where(lane < nx, 0.0, swap_down)

        def line(value, y):
            return jnp.broadcast_to(value[y : y + 1, :], (8, LANES))

        for y in range(yl_n):
            p = line(here, y)
            others = (
                line(x_up, y),
                line(x_down, y),
                line(here, y + 1) if y + 1 < yl_n else line(swap_up, 0),
                line(here, y - 1) if y > 0 else line(swap_down, yl_n - 1),
                line(after, y),
                line(before, y),
            )
            at = pl.ds(pl.multiple_of((e * yl_n + y) * LANES, LANES), LANES)
            diag = line(here, yl_n + y)
            for k, q in enumerate(others):
                both = p * q
                weight = jnp.where(both > 0.0, 2.0 * both / jnp.where(both > 0.0, p + q, 1.0), 0.0)
                coef[1 + k, :, at] = weight
                diag = diag + weight
            coef[0, :, at] = diag
            coef[7, :, at] = jnp.where(diag > 0.0, 1.0 / jnp.where(diag > 0.0, diag, 1.0), 0.0)
            big[0:8, at] = ext[:, pl.ds(pl.multiple_of(((e + 1) * per + y) * LANES, LANES), LANES)]
        return 0

    lax.fori_loop(0, span, fill, 0)

    first, steps = chebyshev_steps()

    def spot(e, y):
        if isinstance(e, int):
            return pl.ds((e * yl_n + y) * LANES, LANES)
        return pl.ds(pl.multiple_of((e * yl_n + y) * LANES, LANES), LANES)

    def stencil(field, e):
        here = [field[:, spot(e, y)] for y in range(yl_n)]
        outs = []
        for y in range(yl_n):
            at = spot(e, y)
            f = here[y]
            y_up = here[y + 1] if y + 1 < yl_n else pltpu.roll(here[0], LANES - nx, 1)
            y_down = here[y - 1] if y > 0 else pltpu.roll(here[yl_n - 1], nx, 1)
            acc = coef[0, :, at] * f
            acc = acc - coef[1, :, at] * pltpu.roll(f, LANES - 1, 1)
            acc = acc - coef[2, :, at] * pltpu.roll(f, 1, 1)
            acc = acc - coef[3, :, at] * y_up
            acc = acc - coef[4, :, at] * y_down
            acc = acc - coef[5, :, at] * field[:, spot(e + 1, y)]
            acc = acc - coef[6, :, at] * field[:, spot(e - 1, y)]
            outs.append(acc)
        return here, outs

    def sweep(lo, hi, work, chunk=4):
        turns = (hi - lo) // chunk

        def one(k, _):
            work([lo + k * chunk + n for n in range(chunk)])
            return 0

        lax.fori_loop(0, turns, one, 0)
        if lo + turns * chunk < hi:
            work(list(range(lo + turns * chunk, hi)))

    def precondition_ref(load):
        def begin(es):
            for e in es:
                for y in range(yl_n):
                    at = spot(e, y)
                    v = load(at)
                    d = coef[7, :, at] * v * first
                    rem[:, at] = v
                    d0[:, at] = d
                    sol[:, at] = d

        sweep(0, span, begin)
        source, target = d0, d1
        for t, (keep, gain) in enumerate(steps):
            def one(es, source=source, target=target, keep=keep, gain=gain):
                found = [stencil(source, e) for e in es]
                for e, (here, outs) in zip(es, found):
                    for y in range(yl_n):
                        at = spot(e, y)
                        r = rem[:, at] - outs[y]
                        rem[:, at] = r
                        d = keep * here[y] + gain * (coef[7, :, at] * r)
                        target[:, at] = d
                        sol[:, at] = sol[:, at] + d

            sweep(t + 1, span - t - 1, one)
            source, target = target, source

    summed = reduce_end(0, begun)
    lead_mat = jnp.where(lane < 8, summed, 0.0) + jnp.where(lane == row + 64, 1.0, 0.0)
    done = eliminate(lead_mat, 8, False)
    lead_t = jnp.where(lane < 8, done, 0.0)
    inverse = pltpu.roll(done, 64, 1)
    big[8:16, :] = full(((1,), (0,)), inverse[:, 0:8], big[0:8, :])

    side = halo * tile
    for j in range(ITERS):
        r = j + 1
        base = 8 * (j + 1)
        precondition_ref(lambda at, base=base: big[base : base + 8, at])

        def apply(es):
            for e in es:
                _, outs = stencil(sol, e)
                for y in range(yl_n):
                    big[0:8, spot(e, y)] = outs[y]

        sweep(halo, halo + zl, apply)
        moves = []
        if j < ITERS - 1:
            moves = [
                remote(big.at[0:8, own_hi - side : own_hi], near_lo.at[j], halo_send.at[j, 0], halo_recv.at[j, 0], dev(nxt)),
                remote(big.at[0:8, own_lo : own_lo + side], near_hi.at[j], halo_send.at[j, 1], halo_recv.at[j, 1], dev(prv)),
            ]
        width = 8 * (j + 2)
        begun = reduce_begin(r, products(j + 2))
        for m in moves:
            m.start()
        summed = reduce_end(r, begun)
        only = jnp.where(lane >= 8, summed, 0.0)
        tmp[...] = only + jnp.where(lane == row + 64, 1.0, 0.0)
        tmp[:, 0:8] = summed[:, 0:8] - full(((1,), (1,)), only, only)
        done = eliminate(tmp[...], 8, False)
        hess[8 * j : 8 * j + 8, :] = jnp.where(lane < base, pltpu.roll(summed, LANES - 8, 1), 0.0)
        hess[8 * j : 8 * j + 8, base : base + 8] = done.T[0:8, :]
        if j < ITERS - 1:
            for m in moves:
                m.wait()
            big[0:8, 0:own_lo] = near_lo[j]
            big[0:8, own_hi : own_hi + side] = near_hi[j]
            mixer = jnp.where(lane < 8, pltpu.roll(done, 64, 1), -done)
            big[base + 8 : base + 16, :] = full(((1,), (0,)), mixer[:, 0:width], big[0:width, :])

    rows = 8 * ITERS
    h = hess[...]
    normal[...] = jnp.zeros_like(normal)
    normal[:, 0:rows] = full(((1,), (1,)), h, h)
    normal[:, rows : rows + 8] = full(((1,), (0,)), h[:, 0:8], lead_t[:, 0:8])
    solved = eliminate(normal[...], rows, True)
    mix = solved.T[rows : rows + 8, :]
    big[0:8, :] = full(((1,), (0,)), mix, big[8 : 8 + rows, :])
    precondition_ref(lambda at: big[0:8, at])

    def finish(es):
        for e in es:
            _, outs = stencil(sol, e)
            for y in range(yl_n):
                k = pl.multiple_of(((e - halo) * yl_n + y) * LANES, LANES)
                w = pl.multiple_of(((e - halo) * yl_n + y) * 8, 8)
                out_ref[0, pl.ds(w, 8), :] = sol[:, spot(e, y)]
                out_ref[1, pl.ds(w, 8), :] = start_own[:, pl.ds(k, LANES)] - outs[y]

    sweep(halo, halo + zl, finish)
    for f in range(2):
        raw_ref[0 : zl * yl_n * 8, :] = full(((1,), (1,)), out_ref[f], pick_ref[...])
        for y in range(yl_n):
            items = [raw_ref[pl.ds(y * 8 + i, zl, stride=yl_n * 8), :] for i in range(nsub)]
            for i, value in enumerate(butterfly(items)):
                out_buf[i, f * yl_n + y] = value
    leaving = []
    for d in range(1, nsub):
        peer = lax.rem(sub + d, nsub)
        c = remote(out_buf.at[peer], out_got.at[:, rows_of(sub), :], out_send.at[d], out_recv.at[sub], {"sub": peer})
        c.start()
        leaving.append(c)
    out_got[:, rows_of(sub), :] = out_buf[sub]
    for d in range(1, nsub):
        peer = lax.rem(sub + d, nsub)
        remote(out_buf.at[peer], out_got.at[:, rows_of(peer), :], out_send.at[d], out_recv.at[peer], {"sub": peer}).wait_recv()
    for f, ref in enumerate((out0_ref, out1_ref)):
        for y in range(yl_n):
            ref[pl.ds(y, LANES, stride=yl_n), :] = out_got[f * yl_n + y].T
    for c in arrivals + leaving:
        c.wait_send()


def fast_body(rhs, perm, accum, counts):
    nsub, nslab = lax.axis_size("sub"), lax.axis_size("slab")
    s, depth, cy, zs = rhs.shape
    nx = depth * nsub
    pack = LANES // nx
    yl = cy // pack
    zl = zs // nsub
    span = zl + 2 * DEG
    pad = DEG + 1

    wide = span * yl * LANES
    f32 = jnp.float32
    rounds = ITERS + 1
    side = DEG * yl * LANES
    dma = pltpu.SemaphoreType.DMA
    out = pl.pallas_call(
        functools.partial(kernel, (nsub, nslab, zl, yl, pack, nx)),
        out_shape=[jax.ShapeDtypeStruct((s * depth * cy, zs), f32)] * 2,
        in_specs=[pl.BlockSpec(memory_space=pltpu.VMEM)] * 3 + [pl.BlockSpec(memory_space=pltpu.SMEM)],
        out_specs=[pl.BlockSpec(memory_space=pltpu.VMEM)] * 2,
        scratch_shapes=[
            pltpu.VMEM((LANES, LANES), f32),
            pltpu.VMEM((zl * (yl + 1) * s, LANES), f32),
            pltpu.VMEM((2, zl * yl * s, LANES), f32),
            pltpu.VMEM((yl + 1, zs, LANES), f32),
            pltpu.VMEM((nsub, yl + 1, zl, LANES), f32),
            pltpu.VMEM((nsub, 2 * yl, zl, LANES), f32),
            pltpu.VMEM((2 * yl, zs, LANES), f32),
            pltpu.VMEM((8, (zl + 2 * pad) * (yl + 1) * LANES), f32),
            pltpu.VMEM((8, 8, wide), f32),
            pltpu.VMEM((8 * (ITERS + 1), wide), f32),
            pltpu.VMEM((ITERS - 1, 8, side), f32),
            pltpu.VMEM((ITERS - 1, 8, side), f32),
            pltpu.VMEM((8, wide), f32),
            pltpu.VMEM((8, wide), f32),
            pltpu.VMEM((8, wide), f32),
            pltpu.VMEM((8, wide), f32),
            pltpu.VMEM((8, zl * yl * LANES), f32),
            pltpu.VMEM((rounds, 8, LANES), f32),
            pltpu.VMEM((rounds, nslab, 8, LANES), f32),
            pltpu.VMEM((rounds, 8, LANES), f32),
            pltpu.VMEM((rounds, nsub, 8, LANES), f32),
            pltpu.VMEM((8, LANES), f32),
            pltpu.VMEM((8 * ITERS, LANES), f32),
            pltpu.VMEM((8 * ITERS, LANES), f32),
            dma((nsub,)),
            dma((nsub,)),
            dma((nsub,)),
            dma((nsub,)),
            dma((2,)),
            dma((2,)),
            dma((ITERS - 1, 2)),
            dma((ITERS - 1, 2)),
            dma((rounds, nslab)),
            dma((rounds, nslab)),
            dma((rounds, nsub)),
            dma((rounds, nsub)),
        ],
        compiler_params=pltpu.CompilerParams(
            collective_id=0, has_side_effects=True, vmem_limit_bytes=48 * 1024 * 1024
        ),
    )(rhs.reshape(-1, zs), perm.reshape(-1, zs), accum.reshape(-1, zs), counts)
    return out[0].reshape(rhs.shape), out[1].reshape(rhs.shape)


def choose(rhs, perm, accum, counts):
    nsub = lax.axis_size("sub")
    s, depth, cy, zs = rhs.shape
    nx = depth * nsub
    fits = s == S == nsub == 8 and zs == LANES and zs // nsub % 8 == 0 and LANES % nx == 0 and zs % nsub == 0 and zs // nsub > DEG
    fits = fits and cy % max(LANES // nx, 1) == 0 and cy // max(LANES // nx, 1) == 4
    if fits:
        return fast_body(rhs, perm, accum, counts)
    return body(rhs, perm, accum, counts)


def solution(mesh):
    placed = (P(None, "sub", None, "slab"), P("sub", None, "slab"), P("sub", None, "slab"), P())
    return jax.shard_map(
        choose,
        mesh=mesh,
        in_specs=placed,
        out_specs=(P(None, "sub", None, "slab"), P(None, "sub", None, "slab")),
        check_vma=False,
    )
```

profile of v0, /device:TPU:0, one launch (start us, length us, event | category | flops | bytes accessed | tf_op | source)
XLA Modules:
  0.0 102.2 jit_solution(17180614961124956760)
XLA Ops:
  0.6 0.0 copy-start.3
  0.6 0.6 copy-done.3
  1.3 0.0 copy-start
  1.3 0.9 copy-done
  2.2 0.0 copy-start.1
  2.2 0.8 copy-done.1
  3.0 0.0 copy-start.2
  3.0 0.8 copy-done.2
  3.8 97.0 %shard_map.59 = (f32[512,128]{1,0:T(8,128)S(1)}, f32[512,128]{1,0:T(8,128)S(1)}) custom-call(f32[512,128]{1,0:T(8,128)S(1)} %bitcast.5, f32[64,128]{1,0:T(8,128)S(1)} %bitcast.8, f32[64,128]{1,0:T(8,128)S(1)} %bitcast.9, s32[8]{0:T(128)S(1)} %copy-done.3), custom_call_target="tpu_custom_call" | custom-call | tf_op jit(solution)/shard_map/pallas_call | solution.py:606
  100.8 0.7 copy.8
  101.5 0.7 copy.9
Async XLA Ops:
  0.6 0.7 copy-start.3
  1.3 0.9 copy-start
  2.2 0.8 copy-start.1
  3.0 0.8 copy-start.2
where the time goes:
time: 103 us; the launch traced here: 102 us
  Pallas kernels  97 us (94%)
  local copies, waits for them, and re-layouts  4.52 us (4%)
    pallas_call x1, Pallas kernels, fast_body(): pl.pallas_call(functools.partial(kernel, (nsub, nslab, zl, yl, pack, nx))...  97 us
    unnamed x10, local copies, waits for them, and re-layouts  4.52 us

commit v1 on v0

--- a/solution.py
+++ b/solution.py
@@ -180,6 +180,9 @@
     return 1.0 / theta, steps
 
 
+CHUNK = 6
+
+
 def eliminate(mat, rows, jordan):
     row = lax.broadcasted_iota(jnp.int32, mat.shape, 0)
     for k in range(rows):
@@ -197,16 +200,20 @@
     return mat
 
 
+SPREAD = 0.52
+REACH = 2
+
+
 def kernel(
     dims,
     rhs_ref, perm_ref, accum_ref, counts_ref, out0_ref, out1_ref,
     pick_ref, raw_ref, out_ref, in_buf, in_got, out_buf, out_got,
-    ext, coef, big, near_lo, near_hi, d0, d1, rem, sol, start_own,
-    part, got1, mid, got2, tmp, hess, normal,
+    ext, coef, inv, diag_own, basis, big, found, d1, d2, d3, rem,
+    part, got1, mid, got2, square, normal,
     in_send, in_recv, out_send, out_recv, xs_send, xs_recv, halo_send, halo_recv, s1_send, s1_recv, s2_send, s2_recv,
 ):
     nsub, nslab, zl, yl_n, pack, nx = dims
-    halo = DEG
+    halo = DEG * REACH
     pad = halo + 1
     span = zl + 2 * halo
     per = yl_n + 1
@@ -248,6 +255,38 @@
         )
 
     group = pack * (LANES // (pack * nsub))
+    pieces = [ref[pl.ds(y, group, stride=yl_n), :] for ref in (perm_ref, accum_ref) for y in range(yl_n)]
+    in_buf[yl_n] = jnp.concatenate(pieces, axis=0).T
+    for y in range(yl_n):
+        in_buf[y] = rhs_ref[pl.ds(y, LANES, stride=yl_n), :].T
+
+    pl.semaphore_wait(barrier, nslab + nsub)
+
+    def rows_of(i):
+        return pl.ds(pl.multiple_of(position(i) * zl, 8), zl)
+
+    halves = ((yl_n, 1), (0, yl_n))
+    arrivals = []
+    for k, (t, n) in enumerate(halves):
+        for d in range(1, nsub):
+            peer = lax.rem(sub + d, nsub)
+            c = remote(
+                in_buf.at[t : t + n, rows_of(peer), :], in_got.at[sub, t : t + n],
+                in_send.at[k, d], in_recv.at[k, sub], {"sub": peer},
+            )
+            c.start()
+            arrivals.append(c)
+    in_got[sub] = in_buf[:, rows_of(sub), :]
+
+    def arrived(k):
+        t, n = halves[k]
+        for d in range(1, nsub):
+            peer = lax.rem(sub + d, nsub)
+            remote(
+                in_buf.at[t : t + n, rows_of(peer), :], in_got.at[peer, t : t + n],
+                in_send.at[k, d], in_recv.at[k, peer], {"sub": peer},
+            ).wait_recv()
+
     wide_row = lax.broadcasted_iota(jnp.int32, (LANES, LANES), 0)
     wide_lane = lax.broadcasted_iota(jnp.int32, (LANES, LANES), 1)
     rank = lax.rem(wide_row, group) // pack
@@ -262,27 +301,7 @@
         before = before + live
     goal = base_of + rank + lax.rem(wide_row, pack) * nx
     pick_ref[...] = jnp.where((rank < live_of) & (goal == wide_lane), 1.0, 0.0).astype(jnp.float32)
-
-    for y in range(yl_n):
-        in_buf[y] = rhs_ref[pl.ds(y, LANES, stride=yl_n), :].T
-    pieces = [ref[pl.ds(y, group, stride=yl_n), :] for ref in (perm_ref, accum_ref) for y in range(yl_n)]
-    in_buf[yl_n] = jnp.concatenate(pieces, axis=0).T
-
-    pl.semaphore_wait(barrier, nslab + nsub)
-
-    def rows_of(i):
-        return pl.ds(pl.multiple_of(position(i) * zl, 8), zl)
-
-    arrivals = []
-    for d in range(1, nsub):
-        peer = lax.rem(sub + d, nsub)
-        c = remote(in_buf.at[:, rows_of(peer), :], in_got.at[sub], in_send.at[d], in_recv.at[sub], {"sub": peer})
-        c.start()
-        arrivals.append(c)
-    in_got[sub] = in_buf[:, rows_of(sub), :]
-    for d in range(1, nsub):
-        peer = lax.rem(sub + d, nsub)
-        remote(in_buf.at[:, rows_of(peer), :], in_got.at[peer], in_send.at[d], in_recv.at[peer], {"sub": peer}).wait_recv()
+    square[...] = jnp.zeros_like(square)
 
     strip = lax.broadcasted_iota(jnp.int32, (zl, LANES), 1) // group
 
@@ -300,40 +319,62 @@
             d //= 2
         return items
 
-    for t in range(per):
-        for i, value in enumerate(butterfly([in_got[i, t] for i in range(nsub)])):
-            raw_ref[pl.ds(t * 8 + i, zl, stride=per * 8), :] = value
-
-    packed = full(((1,), (0,)), raw_ref[...], pick_ref[...])
-    for k in range(zl * per):
-        at = (pad * per + k) * LANES
+    lane = lax.broadcasted_iota(jnp.int32, (8, LANES), 1)
+    row = lax.broadcasted_iota(jnp.int32, (8, LANES), 0)
+    tile = yl_n * LANES
+    side = halo * tile
+    own_lo, own_hi = side, side + zl * tile
+
+    arrived(0)
+    for i, value in enumerate(butterfly([in_got[i, yl_n] for i in range(nsub)])):
+        raw_ref[pl.ds(i, zl, stride=8), :] = value
+    packed = full(((1,), (0,)), raw_ref[0 : zl * 8, :], pick_ref[...])
+    for k in range(zl):
+        at = (pad + k) * LANES
         ext[:, at : at + LANES] = packed[k * 8 : k * 8 + 8, :]
-    edge = pad * per * LANES
-    whole = zl * per * LANES
+    edge = pad * LANES
+    whole = zl * LANES
     up = remote(ext.at[:, whole : whole + edge], ext.at[:, 0:edge], xs_send.at[0], xs_recv.at[0], dev(nxt))
     down = remote(ext.at[:, edge : 2 * edge], ext.at[:, edge + whole : 2 * edge + whole], xs_send.at[1], xs_recv.at[1], dev(prv))
     up.start()
     down.start()
 
-    lane = lax.broadcasted_iota(jnp.int32, (8, LANES), 1)
-    row = lax.broadcasted_iota(jnp.int32, (8, LANES), 0)
-    tile = yl_n * LANES
-    own_lo, own_hi = halo * tile, (halo + zl) * tile
-
-    for k in range(zl):
-        a = (pad + k) * per * LANES
-        start_own[:, k * tile : (k + 1) * tile] = ext[:, a : a + tile]
-        big[0:8, (halo + k) * tile : (halo + k + 1) * tile] = ext[:, a : a + tile]
-
-    def products(blocks):
+    arrived(1)
+    for t in range(yl_n):
+        for i, value in enumerate(butterfly([in_got[i, t] for i in range(nsub)])):
+            raw_ref[pl.ds(t * 8 + i, zl, stride=yl_n * 8), :] = value
+    packed = full(((1,), (0,)), raw_ref[...], pick_ref[...])
+    for k in range(zl * yl_n):
+        basis[0, :, own_lo + k * LANES : own_lo + (k + 1) * LANES] = packed[k * 8 : k * 8 + 8, :]
+        big[0:8, k * LANES : (k + 1) * LANES] = packed[k * 8 : k * 8 + 8, :]
+
+    def swap(n, m):
+        return [
+            remote(
+                basis.at[n, :, own_hi - side : own_hi], basis.at[n, :, 0:side],
+                halo_send.at[m, 0], halo_recv.at[m, 0], dev(nxt),
+            ),
+            remote(
+                basis.at[n, :, own_lo : own_lo + side], basis.at[n, :, own_hi : own_hi + side],
+                halo_send.at[m, 1], halo_recv.at[m, 1], dev(prv),
+            ),
+        ]
+
+    first_swap = swap(0, 0)
+    for c in first_swap:
+        c.start()
+
+    def products(j):
+        blocks = j + 1
+
         def add(k, accs):
             accs = list(accs)
             for h in range(2):
-                at = pl.ds(pl.multiple_of((2 * k + h) * LANES + own_lo, LANES), LANES)
-                w = big[0:8, at]
+                at = pl.ds(pl.multiple_of((2 * k + h) * LANES, LANES), LANES)
+                w = big[8 * j : 8 * j + 8, at]
                 turned = [w] + [pltpu.roll(w, n, 0) for n in range(1, 8)]
                 for b in range(blocks):
-                    v = w if b == 0 else big[8 * b : 8 * b + 8, at]
+                    v = w if b == j else big[8 * b : 8 * b + 8, at]
                     for n in range(8):
                         accs[8 * b + n] = accs[8 * b + n] + v * turned[n]
             return tuple(accs)
@@ -349,18 +390,18 @@
                 out = jnp.where(lane == 8 * b + lax.rem(row + n, 8), line, out)
         return out
 
+    sends = []
+
     def reduce_begin(r, gram):
         part[r] = gram
         got1[r, slab] = part[r]
-        copies = []
         for d in range(1, nslab):
             peer = lax.rem(slab + d, nslab)
             c = remote(part.at[r], got1.at[r, slab], s1_send.at[r, d], s1_recv.at[r, slab], {"slab": peer})
             c.start()
-            copies.append(c)
-        return copies
-
-    def reduce_end(r, copies):
+            sends.append(c)
+
+    def reduce_middle(r):
         for d in range(1, nslab):
             peer = lax.rem(slab + d, nslab)
             remote(part.at[r], got1.at[r, peer], s1_send.at[r, d], s1_recv.at[r, peer], {"slab": peer}).wait_recv()
@@ -373,33 +414,31 @@
             peer = lax.rem(sub + d, nsub)
             c = remote(mid.at[r], got2.at[r, sub], s2_send.at[r, d], s2_recv.at[r, sub], {"sub": peer})
             c.start()
-            copies.append(c)
+            sends.append(c)
+
+    def reduce_end(r):
         for d in range(1, nsub):
             peer = lax.rem(sub + d, nsub)
             remote(mid.at[r], got2.at[r, peer], s2_send.at[r, d], s2_recv.at[r, peer], {"sub": peer}).wait_recv()
         acc = got2[r, 0]
         for i in range(1, nsub):
             acc = acc + got2[r, i]
-        for c in copies:
-            c.wait_send()
         return acc
-
-    begun = reduce_begin(0, products(1))
 
     up.wait()
     down.wait()
     low = jnp.where(place == 0, 0.0, 1.0).astype(jnp.float32)
     high = jnp.where(place == total - 1, 0.0, 1.0).astype(jnp.float32)
     for k in range(pad):
-        a = (k * per + yl_n) * LANES
+        a = k * LANES
         ext[:, a : a + LANES] = ext[:, a : a + LANES] * low
-        b = ((pad + zl + k) * per + yl_n) * LANES
+        b = (pad + zl + k) * LANES
         ext[:, b : b + LANES] = ext[:, b : b + LANES] * high
     along = lax.rem(lane, nx)
 
     def fill(e, _):
         def grab(t):
-            return ext[:, pl.ds(pl.multiple_of(((e + 1 + t) * per + yl_n) * LANES, LANES), LANES)]
+            return ext[:, pl.ds(pl.multiple_of((e + 1 + t) * LANES, LANES), LANES)]
 
         here, after, before = grab(0), grab(1), grab(-1)
         swap_up = pltpu.roll(here, LANES - nx, 1)
@@ -424,17 +463,32 @@
             )
             at = pl.ds(pl.multiple_of((e * yl_n + y) * LANES, LANES), LANES)
             diag = line(here, yl_n + y)
-            for k, q in enumerate(others):
+            weights = []
+            for q in others:
                 both = p * q
                 weight = jnp.where(both > 0.0, 2.0 * both / jnp.where(both > 0.0, p + q, 1.0), 0.0)
-                coef[1 + k, :, at] = weight
+                weights.append(weight)
                 diag = diag + weight
-            coef[0, :, at] = diag
-            coef[7, :, at] = jnp.where(diag > 0.0, 1.0 / jnp.where(diag > 0.0, diag, 1.0), 0.0)
-            big[0:8, at] = ext[:, pl.ds(pl.multiple_of(((e + 1) * per + y) * LANES, LANES), LANES)]
+            over = jnp.where(diag > 0.0, 1.0 / jnp.where(diag > 0.0, diag, 1.0), 0.0)
+            for k, weight in enumerate(weights):
+                coef[k, :, at] = weight * over
+            inv[:, at] = over
+            diag_own[:, at] = diag
         return 0
 
     lax.fori_loop(0, span, fill, 0)
+
+    reduce_begin(0, products(0))
+    for c in first_swap:
+        c.wait()
+
+    def scale(k, _):
+        for h in range(yl_n):
+            at = pl.ds(pl.multiple_of((k * yl_n + h) * LANES, LANES), LANES)
+            basis[0, :, at] = basis[0, :, at] * inv[:, at]
+        return 0
+
+    lax.fori_loop(0, span, scale, 0)
 
     first, steps = chebyshev_steps()
 
@@ -443,7 +497,7 @@
             return pl.ds((e * yl_n + y) * LANES, LANES)
         return pl.ds(pl.multiple_of((e * yl_n + y) * LANES, LANES), LANES)
 
-    def stencil(field, e):
+    def beside(field, e):
         here = [field[:, spot(e, y)] for y in range(yl_n)]
         outs = []
         for y in range(yl_n):
@@ -451,122 +505,111 @@
             f = here[y]
             y_up = here[y + 1] if y + 1 < yl_n else pltpu.roll(here[0], LANES - nx, 1)
             y_down = here[y - 1] if y > 0 else pltpu.roll(here[yl_n - 1], nx, 1)
-            acc = coef[0, :, at] * f
-            acc = acc - coef[1, :, at] * pltpu.roll(f, LANES - 1, 1)
-            acc = acc - coef[2, :, at] * pltpu.roll(f, 1, 1)
-            acc = acc - coef[3, :, at] * y_up
-            acc = acc - coef[4, :, at] * y_down
-            acc = acc - coef[5, :, at] * field[:, spot(e + 1, y)]
-            acc = acc - coef[6, :, at] * field[:, spot(e - 1, y)]
+            acc = coef[0, :, at] * pltpu.roll(f, LANES - 1, 1)
+            acc = acc + coef[1, :, at] * pltpu.roll(f, 1, 1)
+            acc = acc + coef[2, :, at] * y_up
+            acc = acc + coef[3, :, at] * y_down
+            acc = acc + coef[4, :, at] * field[:, spot(e + 1, y)]
+            acc = acc + coef[5, :, at] * field[:, spot(e - 1, y)]
             outs.append(acc)
         return here, outs
 
-    def sweep(lo, hi, work, chunk=4):
+    def sweep(lo, hi, work, chunk=CHUNK):
         turns = (hi - lo) // chunk
 
         def one(k, _):
             work([lo + k * chunk + n for n in range(chunk)])
             return 0
 
-        lax.fori_loop(0, turns, one, 0)
+        if turns > 1:
+            lax.fori_loop(0, turns, one, 0)
+        elif turns:
+            work(list(range(lo, lo + chunk)))
         if lo + turns * chunk < hi:
             work(list(range(lo + turns * chunk, hi)))
 
-    def precondition_ref(load):
-        def begin(es):
+    def advance(j):
+        start = basis.at[j]
+        inset = DEG * (j % REACH)
+        fields = (start, d1, d2, d3)
+        for t, (keep, gain) in enumerate(steps):
+            def one(es, t=t, keep=keep, gain=gain):
+                source, target = fields[t], fields[t + 1]
+                for e in es:
+                    here, outs = beside(source, e)
+                    for y in range(yl_n):
+                        at = spot(e, y)
+                        if t == 0:
+                            r = here[y] - first * (here[y] - outs[y])
+                            d = (keep * first) * here[y] + gain * r
+                        else:
+                            r = rem[:, at] - here[y] + outs[y]
+                            d = keep * here[y] + gain * r
+                        rem[:, at] = r
+                        target[:, at] = d
+
+            sweep(inset + t + 1, span - inset - t - 1, one)
+
+        def last(es, own):
             for e in es:
+                here, outs = beside(d3, e)
                 for y in range(yl_n):
                     at = spot(e, y)
-                    v = load(at)
-                    d = coef[7, :, at] * v * first
-                    rem[:, at] = v
-                    d0[:, at] = d
-                    sol[:, at] = d
-
-        sweep(0, span, begin)
-        source, target = d0, d1
-        for t, (keep, gain) in enumerate(steps):
-            def one(es, source=source, target=target, keep=keep, gain=gain):
-                found = [stencil(source, e) for e in es]
-                for e, (here, outs) in zip(es, found):
-                    for y in range(yl_n):
-                        at = spot(e, y)
-                        r = rem[:, at] - outs[y]
-                        rem[:, at] = r
-                        d = keep * here[y] + gain * (coef[7, :, at] * r)
-                        target[:, at] = d
-                        sol[:, at] = sol[:, at] + d
-
-            sweep(t + 1, span - t - 1, one)
-            source, target = target, source
-
-    summed = reduce_end(0, begun)
-    lead_mat = jnp.where(lane < 8, summed, 0.0) + jnp.where(lane == row + 64, 1.0, 0.0)
-    done = eliminate(lead_mat, 8, False)
-    lead_t = jnp.where(lane < 8, done, 0.0)
-    inverse = pltpu.roll(done, 64, 1)
-    big[8:16, :] = full(((1,), (0,)), inverse[:, 0:8], big[0:8, :])
-
-    side = halo * tile
+                    r = rem[:, at] - here[y] + outs[y]
+                    value = r * (1.0 / SPREAD) if j == 0 else r * (2.0 / SPREAD) - basis[j - 1, :, at]
+                    if j + 1 < ITERS:
+                        basis[j + 1, :, at] = value
+                    if own:
+                        to = spot(e - halo, y)
+                        big[8 * (j + 1) : 8 * (j + 2), to] = value * diag_own[:, at]
+                        found[8 * j : 8 * (j + 1), to] = first * start[:, at] + d1[:, at] + d2[:, at] + here[y]
+
+        if inset + DEG < halo:
+            sweep(inset + DEG, halo, lambda es: last(es, False))
+            sweep(halo + zl, span - inset - DEG, lambda es: last(es, False))
+        sweep(halo, halo + zl, lambda es: last(es, True))
+
     for j in range(ITERS):
-        r = j + 1
-        base = 8 * (j + 1)
-        precondition_ref(lambda at, base=base: big[base : base + 8, at])
-
-        def apply(es):
-            for e in es:
-                _, outs = stencil(sol, e)
-                for y in range(yl_n):
-                    big[0:8, spot(e, y)] = outs[y]
-
-        sweep(halo, halo + zl, apply)
+        advance(j)
         moves = []
-        if j < ITERS - 1:
-            moves = [
-                remote(big.at[0:8, own_hi - side : own_hi], near_lo.at[j], halo_send.at[j, 0], halo_recv.at[j, 0], dev(nxt)),
-                remote(big.at[0:8, own_lo : own_lo + side], near_hi.at[j], halo_send.at[j, 1], halo_recv.at[j, 1], dev(prv)),
-            ]
-        width = 8 * (j + 2)
-        begun = reduce_begin(r, products(j + 2))
-        for m in moves:
-            m.start()
-        summed = reduce_end(r, begun)
-        only = jnp.where(lane >= 8, summed, 0.0)
-        tmp[...] = only + jnp.where(lane == row + 64, 1.0, 0.0)
-        tmp[:, 0:8] = summed[:, 0:8] - full(((1,), (1,)), only, only)
-        done = eliminate(tmp[...], 8, False)
-        hess[8 * j : 8 * j + 8, :] = jnp.where(lane < base, pltpu.roll(summed, LANES - 8, 1), 0.0)
-        hess[8 * j : 8 * j + 8, base : base + 8] = done.T[0:8, :]
-        if j < ITERS - 1:
-            for m in moves:
-                m.wait()
-            big[0:8, 0:own_lo] = near_lo[j]
-            big[0:8, own_hi : own_hi + side] = near_hi[j]
-            mixer = jnp.where(lane < 8, pltpu.roll(done, 64, 1), -done)
-            big[base + 8 : base + 16, :] = full(((1,), (0,)), mixer[:, 0:width], big[0:width, :])
+        if (j + 1) % REACH == 0 and j + 1 < ITERS:
+            moves = swap(j + 1, (j + 1) // REACH)
+            for c in moves:
+                c.start()
+        reduce_begin(j + 1, products(j + 1))
+        reduce_middle(j)
+        for c in moves:
+            c.wait()
+    reduce_middle(ITERS)
 
     rows = 8 * ITERS
-    h = hess[...]
-    normal[...] = jnp.zeros_like(normal)
-    normal[:, 0:rows] = full(((1,), (1,)), h, h)
-    normal[:, rows : rows + 8] = full(((1,), (0,)), h[:, 0:8], lead_t[:, 0:8])
+    for r in range(ITERS + 1):
+        square[8 * r : 8 * r + 8, :] = reduce_end(r)
+    turned = square[...].T
+    gram = [
+        jnp.where(lane < 8 * (r + 1), square[8 * r : 8 * r + 8, :], turned[8 * r : 8 * r + 8, :])
+        for r in range(ITERS + 1)
+    ]
+    up_by = jnp.where(lane < 8, SPREAD, 0.5 * SPREAD)
+    down_by = jnp.where(lane < 8, 0.0, 0.5 * SPREAD)
+    for j in range(ITERS):
+        mixed = gram[j] - SPREAD * gram[1] if j == 0 else gram[j] - (0.5 * SPREAD) * (gram[j + 1] + gram[j - 1])
+        both = mixed - up_by * pltpu.roll(mixed, LANES - 8, 1) - down_by * pltpu.roll(mixed, 8, 1)
+        right = pltpu.roll(mixed, rows, 1)
+        normal[8 * j : 8 * j + 8, :] = jnp.where(lane < rows, both, jnp.where(lane < rows + 8, right, 0.0))
     solved = eliminate(normal[...], rows, True)
-    mix = solved.T[rows : rows + 8, :]
-    big[0:8, :] = full(((1,), (0,)), mix, big[8 : 8 + rows, :])
-    precondition_ref(lambda at: big[0:8, at])
-
-    def finish(es):
-        for e in es:
-            _, outs = stencil(sol, e)
-            for y in range(yl_n):
-                k = pl.multiple_of(((e - halo) * yl_n + y) * LANES, LANES)
-                w = pl.multiple_of(((e - halo) * yl_n + y) * 8, 8)
-                out_ref[0, pl.ds(w, 8), :] = sol[:, spot(e, y)]
-                out_ref[1, pl.ds(w, 8), :] = start_own[:, pl.ds(k, LANES)] - outs[y]
-
-    sweep(halo, halo + zl, finish)
+    filled = jnp.concatenate([solved, jnp.zeros((LANES - rows, LANES), jnp.float32)], axis=0)
+    mix = filled.T[rows : rows + 8, :]
+    used = mix - pltpu.roll(mix * up_by, 8, 1) - pltpu.roll(mix * down_by, LANES - 8, 1)
+    answer = full(((1,), (0,)), mix[:, 0:rows], found[...])
+    taken = full(((1,), (0,)), used[:, 0 : rows + 8], big[...])
+    for k in range(zl * yl_n):
+        at = slice(k * LANES, (k + 1) * LANES)
+        out_ref[0, k * 8 : k * 8 + 8, :] = answer[:, at]
+        out_ref[1, k * 8 : k * 8 + 8, :] = big[0:8, at] - taken[:, at]
+
     for f in range(2):
-        raw_ref[0 : zl * yl_n * 8, :] = full(((1,), (1,)), out_ref[f], pick_ref[...])
+        raw_ref[...] = full(((1,), (1,)), out_ref[f], pick_ref[...])
         for y in range(yl_n):
             items = [raw_ref[pl.ds(y * 8 + i, zl, stride=yl_n * 8), :] for i in range(nsub)]
             for i, value in enumerate(butterfly(items)):
@@ -584,7 +627,7 @@
     for f, ref in enumerate((out0_ref, out1_ref)):
         for y in range(yl_n):
             ref[pl.ds(y, LANES, stride=yl_n), :] = out_got[f * yl_n + y].T
-    for c in arrivals + leaving:
+    for c in arrivals + leaving + sends:
         c.wait_send()
 
 
@@ -595,13 +638,14 @@
     pack = LANES // nx
     yl = cy // pack
     zl = zs // nsub
-    span = zl + 2 * DEG
-    pad = DEG + 1
+    halo = DEG * REACH
+    span = zl + 2 * halo
+    pad = halo + 1
 
     wide = span * yl * LANES
+    own = zl * yl * LANES
     f32 = jnp.float32
     rounds = ITERS + 1
-    side = DEG * yl * LANES
     dma = pltpu.SemaphoreType.DMA
     out = pl.pallas_call(
         functools.partial(kernel, (nsub, nslab, zl, yl, pack, nx)),
@@ -610,37 +654,37 @@
         out_specs=[pl.BlockSpec(memory_space=pltpu.VMEM)] * 2,
         scratch_shapes=[
             pltpu.VMEM((LANES, LANES), f32),
-            pltpu.VMEM((zl * (yl + 1) * s, LANES), f32),
+            pltpu.VMEM((zl * yl * s, LANES), f32),
             pltpu.VMEM((2, zl * yl * s, LANES), f32),
             pltpu.VMEM((yl + 1, zs, LANES), f32),
             pltpu.VMEM((nsub, yl + 1, zl, LANES), f32),
             pltpu.VMEM((nsub, 2 * yl, zl, LANES), f32),
             pltpu.VMEM((2 * yl, zs, LANES), f32),
-            pltpu.VMEM((8, (zl + 2 * pad) * (yl + 1) * LANES), f32),
-            pltpu.VMEM((8, 8, wide), f32),
-            pltpu.VMEM((8 * (ITERS + 1), wide), f32),
-            pltpu.VMEM((ITERS - 1, 8, side), f32),
-            pltpu.VMEM((ITERS - 1, 8, side), f32),
+            pltpu.VMEM((8, (zl + 2 * pad) * LANES), f32),
+            pltpu.VMEM((6, 8, wide), f32),
+            pltpu.VMEM((8, wide), f32),
+            pltpu.VMEM((8, wide), f32),
+            pltpu.VMEM((ITERS, 8, wide), f32),
+            pltpu.VMEM((8 * rounds, own), f32),
+            pltpu.VMEM((8 * ITERS, own), f32),
             pltpu.VMEM((8, wide), f32),
             pltpu.VMEM((8, wide), f32),
             pltpu.VMEM((8, wide), f32),
             pltpu.VMEM((8, wide), f32),
-            pltpu.VMEM((8, zl * yl * LANES), f32),
             pltpu.VMEM((rounds, 8, LANES), f32),
             pltpu.VMEM((rounds, nslab, 8, LANES), f32),
             pltpu.VMEM((rounds, 8, LANES), f32),
             pltpu.VMEM((rounds, nsub, 8, LANES), f32),
-            pltpu.VMEM((8, LANES), f32),
+            pltpu.VMEM((LANES, LANES), f32),
             pltpu.VMEM((8 * ITERS, LANES), f32),
-            pltpu.VMEM((8 * ITERS, LANES), f32),
-            dma((nsub,)),
-            dma((nsub,)),
+            dma((2, nsub)),
+            dma((2, nsub)),
             dma((nsub,)),
             dma((nsub,)),
             dma((2,)),
             dma((2,)),
-            dma((ITERS - 1, 2)),
-            dma((ITERS - 1, 2)),
+            dma((ITERS // REACH, 2)),
+            dma((ITERS // REACH, 2)),
             dma((rounds, nslab)),
             dma((rounds, nslab)),
             dma((rounds, nsub)),
@@ -657,7 +701,7 @@
     nsub = lax.axis_size("sub")
     s, depth, cy, zs = rhs.shape
     nx = depth * nsub
-    fits = s == S == nsub == 8 and zs == LANES and zs // nsub % 8 == 0 and LANES % nx == 0 and zs % nsub == 0 and zs // nsub > DEG
+    fits = s == S == nsub == 8 and zs == LANES and zs // nsub % 8 == 0 and LANES % nx == 0 and zs % nsub == 0 and zs // nsub > DEG * REACH
     fits = fits and cy % max(LANES // nx, 1) == 0 and cy // max(LANES // nx, 1) == 4
     if fits:
         return fast_body(rhs, perm, accum, counts)

time: 103 us -> 70.2 us (0.68)
  Pallas kernels: 97 us -> 63.9 us
    pallas_call x1, Pallas kernels: 97 us -> 63.9 us  [fast_body(): pl.pallas_call(functools.partial(kernel, (nsub, nslab, zl, yl, pack, nx))...]
where the time goes in v1:
time: 70.2 us; the launch traced here: 69 us
  Pallas kernels  63.9 us (91%)
  local copies, waits for them, and re-layouts  4.52 us (6%)
    pallas_call x1, Pallas kernels, fast_body(): pl.pallas_call(functools.partial(kernel, (nsub, nslab, zl, yl, pack, nx))...  63.9 us
    unnamed x10, local copies, waits for them, and re-layouts  4.52 us

profile of v1, /device:TPU:0, one launch (start us, length us, event | category | flops | bytes accessed | tf_op | source)
XLA Modules:
  0.0 69.0 jit_solution(18252445440935837344)
XLA Ops:
  0.6 0.0 copy-start.3
  0.6 0.6 copy-done.3
  1.3 0.0 copy-start
  1.3 0.9 %copy-done = f32[8,8,8,128]{3,2,1,0:T(8,128)S(1)} copy-done((f32[8,8,8,128]{3,2,1,0:T(8,128)S(1)}, f32[8,8,8,128]{3,2,1,0:T(8,128)}, u32[]{:S(2)}) %copy-start) | copy-done | bytes 262168
  2.2 0.0 copy-start.1
  2.2 0.8 %copy-done.1 = f32[8,8,128]{2,1,0:T(8,128)S(1)} copy-done((f32[8,8,128]{2,1,0:T(8,128)S(1)}, f32[8,8,128]{2,1,0:T(8,128)}, u32[]{:S(2)}) %copy-start.1) | copy-done | bytes 32792
  3.0 0.0 copy-start.2
  3.0 0.8 %copy-done.2 = f32[8,8,128]{2,1,0:T(8,128)S(1)} copy-done((f32[8,8,128]{2,1,0:T(8,128)S(1)}, f32[8,8,128]{2,1,0:T(8,128)}, u32[]{:S(2)}) %copy-start.2) | copy-done | bytes 32792
  3.8 63.9 %shard_map.59 = (f32[512,128]{1,0:T(8,128)S(1)}, f32[512,128]{1,0:T(8,128)S(1)}) custom-call(f32[512,128]{1,0:T(8,128)S(1)} %bitcast.5, f32[64,128]{1,0:T(8,128)S(1)} %bitcast.8, f32[64,128]{1,0:T(8,128)S(1)} %bitcast.9, s32[8]{0:T(128)S(1)} %copy-done.3), custom_call_target="tpu_custom_call" | custom-call | tf_op jit(solution)/shard_map/pallas_call | solution.py:650
  67.6 0.7 %copy.8 = f32[8,8,8,128]{3,2,1,0:T(8,128)} copy(f32[8,8,8,128]{3,2,1,0:T(8,128)S(1)} %bitcast.7) | data formatting | bytes 524288
  68.3 0.7 %copy.9 = f32[8,8,8,128]{3,2,1,0:T(8,128)} copy(f32[8,8,8,128]{3,2,1,0:T(8,128)S(1)} %bitcast.6) | data formatting | bytes 524288
Async XLA Ops:
  0.6 0.7 copy-start.3
  1.3 0.9 %copy-start = (f32[8,8,8,128]{3,2,1,0:T(8,128)S(1)}, f32[8,8,8,128]{3,2,1,0:T(8,128)}, u32[]{:S(2)}) copy-start(f32[8,8,8,128]{3,2,1,0:T(8,128)} %param.4) | copy-start | bytes 786436
  2.2 0.8 %copy-start.1 = (f32[8,8,128]{2,1,0:T(8,128)S(1)}, f32[8,8,128]{2,1,0:T(8,128)}, u32[]{:S(2)}) copy-start(f32[8,8,128]{2,1,0:T(8,128)} %param.5) | copy-start | bytes 98308
  3.0 0.8 %copy-start.2 = (f32[8,8,128]{2,1,0:T(8,128)S(1)}, f32[8,8,128]{2,1,0:T(8,128)}, u32[]{:S(2)}) copy-start(f32[8,8,128]{2,1,0:T(8,128)} %param.6) | copy-start | bytes 98308

commit v2 on v1

--- a/solution.py
+++ b/solution.py
@@ -180,24 +180,43 @@
     return 1.0 / theta, steps
 
 
-CHUNK = 6
-
-
-def eliminate(mat, rows, jordan):
-    row = lax.broadcasted_iota(jnp.int32, mat.shape, 0)
-    for k in range(rows):
-        column = jnp.broadcast_to(mat[:, k : k + 1], mat.shape)
-        pivot = column[k : k + 1, :]
-        line = mat[k : k + 1, :]
-        if jordan:
-            scaled = line / pivot
-            mat = jnp.where(row == k, scaled, mat - column * scaled)
-        else:
-            root = lax.rsqrt(pivot)
-            root = root * (1.5 - 0.5 * pivot * root * root)
-            scaled = line * root
-            mat = jnp.where(row == k, scaled, jnp.where(row > k, mat - column * root * scaled, mat))
-    return mat
+def spread_rows(value, k):
+    return jnp.broadcast_to(value[k : k + 1, :], value.shape)
+
+
+def spread_lane(value, k):
+    return jnp.broadcast_to(value[:, k : k + 1], value.shape)
+
+
+def times(columns, block):
+    total = columns[0] * spread_rows(block, 0)
+    for c in range(1, 8):
+        total = total + columns[c] * spread_rows(block, c)
+    return total
+
+
+def invert(cols, row):
+    cols = list(cols)
+    for k in range(8):
+        over = 1.0 / spread_rows(cols[k], k)
+        pivot = cols[k]
+        for c in range(8):
+            if c == k:
+                cols[c] = jnp.where(row == k, over, -pivot * over)
+            else:
+                scaled = spread_rows(cols[c], k) * over
+                cols[c] = jnp.where(row == k, scaled, cols[c] - pivot * scaled)
+    return cols
+
+
+def block_jordan(blocks, row):
+    blocks = list(blocks)
+    for k in range(len(blocks)):
+        cols = [[spread_lane(b, 8 * k + c) for c in range(8)] for b in blocks]
+        solved = times(invert(cols[k], row), blocks[k])
+        for i in range(len(blocks)):
+            blocks[i] = solved if i == k else blocks[i] - times(cols[i], solved)
+    return blocks
 
 
 SPREAD = 0.52
@@ -206,10 +225,11 @@
 
 def kernel(
     dims,
-    rhs_ref, perm_ref, accum_ref, counts_ref, out0_ref, out1_ref,
+    rhs_hbm, perm_hbm, accum_hbm, counts_hbm, out0_ref, out1_ref,
+    rhs_ref, perm_ref, accum_ref, counts_ref, load_sem,
     pick_ref, raw_ref, out_ref, in_buf, in_got, out_buf, out_got,
-    ext, coef, inv, diag_own, basis, big, found, d1, d2, d3, rem,
-    part, got1, mid, got2, square, normal,
+    ext, coef, inv, diag_own, first_field, basis, big, found, d1, d2, d3, rem,
+    part, got1, mid, got2, square,
     in_send, in_recv, out_send, out_recv, xs_send, xs_recv, halo_send, halo_recv, s1_send, s1_recv, s2_send, s2_recv,
 ):
     nsub, nslab, zl, yl_n, pack, nx = dims
@@ -235,6 +255,15 @@
         at = at + lax.rem(g // nsub, 2) * (nsub - 1 - 2 * at)
         across = at // (nsub // 2)
         return {"sub": 2 * (at + across * (nsub - 1 - 2 * at)) + across, "slab": g // nsub}
+
+    loads = [
+        pltpu.make_async_copy(src, dst, load_sem.at[k])
+        for k, (src, dst) in enumerate(
+            ((perm_hbm, perm_ref), (accum_hbm, accum_ref), (rhs_hbm, rhs_ref), (counts_hbm, counts_ref))
+        )
+    ]
+    for c in loads:
+        c.start()
 
     barrier = pltpu.get_barrier_semaphore()
     for d in range(1, nslab):
@@ -255,6 +284,9 @@
         )
 
     group = pack * (LANES // (pack * nsub))
+    square[...] = jnp.zeros_like(square)
+    for c in loads:
+        c.wait()
     pieces = [ref[pl.ds(y, group, stride=yl_n), :] for ref in (perm_ref, accum_ref) for y in range(yl_n)]
     in_buf[yl_n] = jnp.concatenate(pieces, axis=0).T
     for y in range(yl_n):
@@ -301,7 +333,6 @@
         before = before + live
     goal = base_of + rank + lax.rem(wide_row, pack) * nx
     pick_ref[...] = jnp.where((rank < live_of) & (goal == wide_lane), 1.0, 0.0).astype(jnp.float32)
-    square[...] = jnp.zeros_like(square)
 
     strip = lax.broadcasted_iota(jnp.int32, (zl, LANES), 1) // group
 
@@ -478,17 +509,12 @@
 
     lax.fori_loop(0, span, fill, 0)
 
-    reduce_begin(0, products(0))
-    for c in first_swap:
-        c.wait()
-
-    def scale(k, _):
-        for h in range(yl_n):
-            at = pl.ds(pl.multiple_of((k * yl_n + h) * LANES, LANES), LANES)
-            basis[0, :, at] = basis[0, :, at] * inv[:, at]
-        return 0
-
-    lax.fori_loop(0, span, scale, 0)
+    def scale(lo, hi):
+        for k in range(lo * yl_n, hi * yl_n):
+            at = slice(k * LANES, (k + 1) * LANES)
+            first_field[:, at] = basis[0, :, at] * inv[:, at]
+
+    scale(halo, halo + zl)
 
     first, steps = chebyshev_steps()
 
@@ -514,72 +540,63 @@
             outs.append(acc)
         return here, outs
 
-    def sweep(lo, hi, work, chunk=CHUNK):
-        turns = (hi - lo) // chunk
-
-        def one(k, _):
-            work([lo + k * chunk + n for n in range(chunk)])
-            return 0
-
-        if turns > 1:
-            lax.fori_loop(0, turns, one, 0)
-        elif turns:
-            work(list(range(lo, lo + chunk)))
-        if lo + turns * chunk < hi:
-            work(list(range(lo + turns * chunk, hi)))
-
-    def advance(j):
-        start = basis.at[j]
+    def field_of(j):
+        return first_field if j == 0 else basis.at[j]
+
+    def advance(j, t, planes):
+        fields = (field_of(j), d1, d2, d3)
+        source = fields[t]
+        for e in planes:
+            here, outs = beside(source, e)
+            for y in range(yl_n):
+                at = spot(e, y)
+                if t < DEG - 1:
+                    keep, gain = steps[t]
+                    if t == 0:
+                        r = here[y] - first * (here[y] - outs[y])
+                        d = (keep * first) * here[y] + gain * r
+                    else:
+                        r = rem[:, at] - here[y] + outs[y]
+                        d = keep * here[y] + gain * r
+                    rem[:, at] = r
+                    fields[t + 1][:, at] = d
+                    continue
+                r = rem[:, at] - here[y] + outs[y]
+                value = r * (1.0 / SPREAD) if j == 0 else r * (2.0 / SPREAD) - field_of(j - 1)[:, at]
+                if j + 1 < ITERS:
+                    basis[j + 1, :, at] = value
+                if halo <= e < halo + zl:
+                    to = spot(e - halo, y)
+                    big[8 * (j + 1) : 8 * (j + 2), to] = value * diag_own[:, at]
+                    found[8 * j : 8 * (j + 1), to] = first * fields[0][:, at] + d1[:, at] + d2[:, at] + here[y]
+
+    moves = first_swap
+    for j in range(ITERS):
         inset = DEG * (j % REACH)
-        fields = (start, d1, d2, d3)
-        for t, (keep, gain) in enumerate(steps):
-            def one(es, t=t, keep=keep, gain=gain):
-                source, target = fields[t], fields[t + 1]
-                for e in es:
-                    here, outs = beside(source, e)
-                    for y in range(yl_n):
-                        at = spot(e, y)
-                        if t == 0:
-                            r = here[y] - first * (here[y] - outs[y])
-                            d = (keep * first) * here[y] + gain * r
-                        else:
-                            r = rem[:, at] - here[y] + outs[y]
-                            d = keep * here[y] + gain * r
-                        rem[:, at] = r
-                        target[:, at] = d
-
-            sweep(inset + t + 1, span - inset - t - 1, one)
-
-        def last(es, own):
-            for e in es:
-                here, outs = beside(d3, e)
-                for y in range(yl_n):
-                    at = spot(e, y)
-                    r = rem[:, at] - here[y] + outs[y]
-                    value = r * (1.0 / SPREAD) if j == 0 else r * (2.0 / SPREAD) - basis[j - 1, :, at]
-                    if j + 1 < ITERS:
-                        basis[j + 1, :, at] = value
-                    if own:
-                        to = spot(e - halo, y)
-                        big[8 * (j + 1) : 8 * (j + 2), to] = value * diag_own[:, at]
-                        found[8 * j : 8 * (j + 1), to] = first * start[:, at] + d1[:, at] + d2[:, at] + here[y]
-
-        if inset + DEG < halo:
-            sweep(inset + DEG, halo, lambda es: last(es, False))
-            sweep(halo + zl, span - inset - DEG, lambda es: last(es, False))
-        sweep(halo, halo + zl, lambda es: last(es, True))
-
-    for j in range(ITERS):
-        advance(j)
-        moves = []
+        if not inset:
+            for t in range(DEG):
+                advance(j, t, range(halo + t + 1, halo + zl - t - 1))
+            reduce_begin(j, products(j))
+            if j:
+                reduce_middle(j - 1)
+            for c in moves:
+                c.wait()
+            if not j:
+                scale(0, halo)
+                scale(halo + zl, span)
+            for t in range(DEG):
+                outer = [*range(t + 1, halo + t + 1), *range(halo + zl - t - 1, span - t - 1)]
+                advance(j, t, outer)
+        else:
+            for t in range(DEG):
+                advance(j, t, range(inset + t + 1, span - inset - t - 1))
         if (j + 1) % REACH == 0 and j + 1 < ITERS:
             moves = swap(j + 1, (j + 1) // REACH)
             for c in moves:
                 c.start()
-        reduce_begin(j + 1, products(j + 1))
-        reduce_middle(j)
-        for c in moves:
-            c.wait()
+        else:
+            reduce_begin(j + 1, products(j + 1))
+            reduce_middle(j)
     reduce_middle(ITERS)
 
     rows = 8 * ITERS
@@ -592,39 +609,50 @@
     ]
     up_by = jnp.where(lane < 8, SPREAD, 0.5 * SPREAD)
     down_by = jnp.where(lane < 8, 0.0, 0.5 * SPREAD)
+    system = []
     for j in range(ITERS):
         mixed = gram[j] - SPREAD * gram[1] if j == 0 else gram[j] - (0.5 * SPREAD) * (gram[j + 1] + gram[j - 1])
         both = mixed - up_by * pltpu.roll(mixed, LANES - 8, 1) - down_by * pltpu.roll(mixed, 8, 1)
         right = pltpu.roll(mixed, rows, 1)
-        normal[8 * j : 8 * j + 8, :] = jnp.where(lane < rows, both, jnp.where(lane < rows + 8, right, 0.0))
-    solved = eliminate(normal[...], rows, True)
-    filled = jnp.concatenate([solved, jnp.zeros((LANES - rows, LANES), jnp.float32)], axis=0)
+        system.append(jnp.where(lane < rows, both, jnp.where(lane < rows + 8, right, 0.0)))
+    solved = block_jordan(system, row)
+    filled = jnp.concatenate([*solved, jnp.zeros((LANES - rows, LANES), jnp.float32)], axis=0)
     mix = filled.T[rows : rows + 8, :]
     used = mix - pltpu.roll(mix * up_by, 8, 1) - pltpu.roll(mix * down_by, LANES - 8, 1)
-    answer = full(((1,), (0,)), mix[:, 0:rows], found[...])
-    taken = full(((1,), (0,)), used[:, 0 : rows + 8], big[...])
-    for k in range(zl * yl_n):
-        at = slice(k * LANES, (k + 1) * LANES)
-        out_ref[0, k * 8 : k * 8 + 8, :] = answer[:, at]
-        out_ref[1, k * 8 : k * 8 + 8, :] = big[0:8, at] - taken[:, at]
+    leaving = []
+
+    def deliver(f, k, peer):
+        return remote(
+            out_buf.at[peer, f * yl_n : (f + 1) * yl_n],
+            out_got.at[f * yl_n : (f + 1) * yl_n, rows_of(sub), :],
+            out_send.at[f, k], out_recv.at[f, sub], {"sub": peer},
+        )
 
     for f in range(2):
+        if f == 0:
+            mixture = full(((1,), (0,)), mix[:, 0:rows], found[...])
+        else:
+            mixture = big[0:8, :] - full(((1,), (0,)), used[:, 0 : rows + 8], big[...])
+        for k in range(zl * yl_n):
+            out_ref[f, k * 8 : k * 8 + 8, :] = mixture[:, k * LANES : (k + 1) * LANES]
         raw_ref[...] = full(((1,), (1,)), out_ref[f], pick_ref[...])
         for y in range(yl_n):
             items = [raw_ref[pl.ds(y * 8 + i, zl, stride=yl_n * 8), :] for i in range(nsub)]
             for i, value in enumerate(butterfly(items)):
                 out_buf[i, f * yl_n + y] = value
-    leaving = []
-    for d in range(1, nsub):
-        peer = lax.rem(sub + d, nsub)
-        c = remote(out_buf.at[peer], out_got.at[:, rows_of(sub), :], out_send.at[d], out_recv.at[sub], {"sub": peer})
-        c.start()
-        leaving.append(c)
-    out_got[:, rows_of(sub), :] = out_buf[sub]
-    for d in range(1, nsub):
-        peer = lax.rem(sub + d, nsub)
-        remote(out_buf.at[peer], out_got.at[:, rows_of(peer), :], out_send.at[d], out_recv.at[peer], {"sub": peer}).wait_recv()
+        for d in range(1, nsub):
+            c = deliver(f, d, lax.rem(sub + d, nsub))
+            c.start()
+            leaving.append(c)
+        out_got[f * yl_n : (f + 1) * yl_n, rows_of(sub), :] = out_buf[sub, f * yl_n : (f + 1) * yl_n]
     for f, ref in enumerate((out0_ref, out1_ref)):
+        for d in range(1, nsub):
+            peer = lax.rem(sub + d, nsub)
+            remote(
+                out_buf.at[peer, f * yl_n : (f + 1) * yl_n],
+                out_got.at[f * yl_n : (f + 1) * yl_n, rows_of(peer), :],
+                out_send.at[f, d], out_recv.at[f, peer], {"sub": peer},
+            ).wait_recv()
         for y in range(yl_n):
             ref[pl.ds(y, LANES, stride=yl_n), :] = out_got[f * yl_n + y].T
     for c in arrivals + leaving + sends:
@@ -650,9 +678,14 @@
     out = pl.pallas_call(
         functools.partial(kernel, (nsub, nslab, zl, yl, pack, nx)),
         out_shape=[jax.ShapeDtypeStruct((s * depth * cy, zs), f32)] * 2,
-        in_specs=[pl.BlockSpec(memory_space=pltpu.VMEM)] * 3 + [pl.BlockSpec(memory_space=pltpu.SMEM)],
+        in_specs=[pl.BlockSpec(memory_space=pltpu.HBM)] * 4,
         out_specs=[pl.BlockSpec(memory_space=pltpu.VMEM)] * 2,
         scratch_shapes=[
+            pltpu.VMEM((s * depth * cy, zs), f32),
+            pltpu.VMEM((depth * cy, zs), f32),
+            pltpu.VMEM((depth * cy, zs), f32),
+            pltpu.SMEM((nsub,), jnp.int32),
+            dma((4,)),
             pltpu.VMEM((LANES, LANES), f32),
             pltpu.VMEM((zl * yl * s, LANES), f32),
             pltpu.VMEM((2, zl * yl * s, LANES), f32),
@@ -662,6 +695,7 @@
             pltpu.VMEM((2 * yl, zs, LANES), f32),
             pltpu.VMEM((8, (zl + 2 * pad) * LANES), f32),
             pltpu.VMEM((6, 8, wide), f32),
+            pltpu.VMEM((8, wide), f32),
             pltpu.VMEM((8, wide), f32),
             pltpu.VMEM((8, wide), f32),
             pltpu.VMEM((ITERS, 8, wide), f32),
@@ -676,11 +710,10 @@
             pltpu.VMEM((rounds, 8, LANES), f32),
             pltpu.VMEM((rounds, nsub, 8, LANES), f32),
             pltpu.VMEM((LANES, LANES), f32),
-            pltpu.VMEM((8 * ITERS, LANES), f32),
             dma((2, nsub)),
             dma((2, nsub)),
-            dma((nsub,)),
-            dma((nsub,)),
+            dma((2, nsub)),
+            dma((2, nsub)),
             dma((2,)),
             dma((2,)),
             dma((ITERS // REACH, 2)),
@@ -691,7 +724,7 @@
             dma((rounds, nsub)),
         ],
         compiler_params=pltpu.CompilerParams(
-            collective_id=0, has_side_effects=True, vmem_limit_bytes=48 * 1024 * 1024
+            collective_id=0, has_side_effects=True, vmem_limit_bytes=60*1024*1024
         ),
     )(rhs.reshape(-1, zs), perm.reshape(-1, zs), accum.reshape(-1, zs), counts)
     return out[0].reshape(rhs.shape), out[1].reshape(rhs.shape)

time: 70.2 us -> 59.4 us (0.85); the launches traced: 69 us -> 59.2 us
  Pallas kernels: 63.9 us -> 56.2 us
  local copies, waits for them, and re-layouts: 4.52 us -> 2.42 us
    pallas_call x1, Pallas kernels: 63.9 us -> 56.2 us  [fast_body(): pl.pallas_call(functools.partial(kernel, (nsub, nslab, zl, yl, pack, nx))...]
    unnamed x10 -> x4, local copies, waits for them, and re-layouts: 4.52 us -> 2.42 us
where the time goes in v2:
time: 59.4 us; the launch traced here: 59.2 us
  Pallas kernels  56.2 us (95%)
  local copies, waits for them, and re-layouts  2.42 us (4%)
  between operations  0.65 us (1%)
    pallas_call x1, Pallas kernels, fast_body(): pl.pallas_call(functools.partial(kernel, (nsub, nslab, zl, yl, pack, nx))...  56.2 us
    unnamed x4, local copies, waits for them, and re-layouts  2.42 us

profile of v2, /device:TPU:0, one launch (start us, length us, event | category | flops | bytes accessed | tf_op | source)
XLA Modules:
  0.0 59.2 jit_solution(8394235632796364526)
XLA Ops:
  0.6 56.2 %shard_map.59 = (f32[512,128]{1,0:T(8,128)}, f32[512,128]{1,0:T(8,128)}) custom-call(f32[512,128]{1,0:T(8,128)} %bitcast.5, f32[64,128]{1,0:T(8,128)} %bitcast.8, f32[64,128]{1,0:T(8,128)} %bitcast.9, s32[8]{0:T(128)} %counts_hbm.1), custom_call_target="tpu_custom_call" | custom-call | tf_op jit(solution)/shard_map/pallas_call | solution.py:678
  56.8 0.0 copy-start
  56.8 1.7 %copy.8 = f32[8,8,8,128]{3,2,1,0:T(8,128)} copy(f32[8,8,8,128]{3,2,1,0:T(8,128)} %bitcast.7) | data formatting | bytes 524288
  58.5 0.0 copy-done
  58.5 0.7 %copy.9 = f32[8,8,8,128]{3,2,1,0:T(8,128)} copy(f32[8,8,8,128]{3,2,1,0:T(8,128)S(1)} %bitcast.6) | data formatting | bytes 524288
Async XLA Ops:
  56.8 1.7 %copy-start = (f32[512,128]{1,0:T(8,128)S(1)}, f32[512,128]{1,0:T(8,128)}, u32[]{:S(2)}) copy-start(f32[512,128]{1,0:T(8,128)} %get-tuple-element.5) | copy-start | bytes 786436

commit v3 on v2

--- a/solution.py
+++ b/solution.py
@@ -227,7 +227,8 @@
     dims,
     rhs_hbm, perm_hbm, accum_hbm, counts_hbm, out0_ref, out1_ref,
     rhs_ref, perm_ref, accum_ref, counts_ref, load_sem,
-    pick_ref, raw_ref, out_ref, in_buf, in_got, out_buf, out_got,
+    pick_ref, ends_ref, raw_ref, out_ref, flux_ref, in_buf, in_got, out_buf, out_got, rim_buf, rim_got,
+    wall, edge_ref,
     ext, coef, inv, diag_own, first_field, basis, big, found, d1, d2, d3, rem,
     part, got1, mid, got2, square,
     in_send, in_recv, out_send, out_recv, xs_send, xs_recv, halo_send, halo_recv, s1_send, s1_recv, s2_send, s2_recv,
@@ -240,21 +241,22 @@
     sub = lax.axis_index("sub")
     slab = lax.axis_index("slab")
 
-    def position(i):
-        across = lax.rem(i, 2)
-        at = i // 2 + across * (nsub - 1 - 2 * (i // 2))
-        return at + lax.rem(slab, 2) * (nsub - 1 - 2 * at)
-
-    place = slab * nsub + position(sub)
     total = nsub * nslab
+    layer, core = slab // 2, lax.rem(slab, 2)
+    at = sub // 2 + lax.rem(sub, 2) * (nsub - 1 - 2 * (sub // 2))
+    at = at + lax.rem(layer, 2) * (nsub - 1 - 2 * at)
+    place = 2 * (layer * nsub + at) + core
+    home, mine = place // nsub, lax.rem(place, nsub)
     nxt = lax.rem(place + 1, total)
     prv = lax.rem(place + total - 1, total)
 
     def dev(g):
-        at = lax.rem(g, nsub)
-        at = at + lax.rem(g // nsub, 2) * (nsub - 1 - 2 * at)
+        chip = g // 2
+        layer = chip // nsub
+        at = lax.rem(chip, nsub)
+        at = at + lax.rem(layer, 2) * (nsub - 1 - 2 * at)
         across = at // (nsub // 2)
-        return {"sub": 2 * (at + across * (nsub - 1 - 2 * at)) + across, "slab": g // nsub}
+        return {"sub": 2 * (at + across * (nsub - 1 - 2 * at)) + across, "slab": 2 * layer + lax.rem(g, 2)}
 
     loads = [
         pltpu.make_async_copy(src, dst, load_sem.at[k])
@@ -266,16 +268,11 @@
         c.start()
 
     barrier = pltpu.get_barrier_semaphore()
-    for d in range(1, nslab):
-        pl.semaphore_signal(
-            barrier, inc=1, device_id={"slab": lax.rem(slab + d, nslab)}, device_id_type=pl.DeviceIdType.MESH
-        )
+    peers = [{"slab": lax.rem(slab + d, nslab)} for d in range(1, nslab)]
     for d in range(1, nsub):
-        pl.semaphore_signal(
-            barrier, inc=1, device_id={"sub": lax.rem(sub + d, nsub)}, device_id_type=pl.DeviceIdType.MESH
-        )
-    for g in (nxt, prv):
-        pl.semaphore_signal(barrier, inc=1, device_id=dev(g), device_id_type=pl.DeviceIdType.MESH)
+        peers += [{"sub": lax.rem(sub + d, nsub)}, {"sub": lax.rem(sub + d, nsub), "slab": 2 * layer + 1 - core}]
+    for device in peers:
+        pl.semaphore_signal(barrier, inc=1, device_id=device, device_id_type=pl.DeviceIdType.MESH)
 
     def remote(src, dst, send, recv, device):
         return pltpu.make_async_remote_copy(
@@ -292,32 +289,36 @@
     for y in range(yl_n):
         in_buf[y] = rhs_ref[pl.ds(y, LANES, stride=yl_n), :].T
 
-    pl.semaphore_wait(barrier, nslab + nsub)
+    pl.semaphore_wait(barrier, len(peers))
 
     def rows_of(i):
-        return pl.ds(pl.multiple_of(position(i) * zl, 8), zl)
+        return pl.ds(pl.multiple_of(i * zl, 8), zl)
 
     halves = ((yl_n, 1), (0, yl_n))
     arrivals = []
     for k, (t, n) in enumerate(halves):
-        for d in range(1, nsub):
-            peer = lax.rem(sub + d, nsub)
+        for d in range(nsub):
+            q = lax.rem(mine + d, nsub)
+            goal = slab * nsub + q
             c = remote(
-                in_buf.at[t : t + n, rows_of(peer), :], in_got.at[sub, t : t + n],
-                in_send.at[k, d], in_recv.at[k, sub], {"sub": peer},
+                in_buf.at[t : t + n, rows_of(q), :], in_got.at[sub, t : t + n],
+                in_send.at[k, d], in_recv.at[k, sub], dev(goal),
             )
-            c.start()
-            arrivals.append(c)
-    in_got[sub] = in_buf[:, rows_of(sub), :]
+            pl.when(goal != place)(c.start)
+            arrivals.append((goal != place, c))
+
+    @pl.when(home == slab)
+    def _():
+        in_got[sub] = in_buf[:, rows_of(mine), :]
 
     def arrived(k):
         t, n = halves[k]
-        for d in range(1, nsub):
-            peer = lax.rem(sub + d, nsub)
-            remote(
-                in_buf.at[t : t + n, rows_of(peer), :], in_got.at[peer, t : t + n],
-                in_send.at[k, d], in_recv.at[k, peer], {"sub": peer},
-            ).wait_recv()
+        for i in range(nsub):
+            c = remote(
+                in_buf.at[t : t + n, 0:zl, :], in_got.at[i, t : t + n],
+                in_send.at[k, i], in_recv.at[k, i], {"sub": i, "slab": home},
+            )
+            pl.when((home != slab) | (sub != i))(c.wait_recv)
 
     wide_row = lax.broadcasted_iota(jnp.int32, (LANES, LANES), 0)
     wide_lane = lax.broadcasted_iota(jnp.int32, (LANES, LANES), 1)
@@ -334,6 +335,37 @@
     goal = base_of + rank + lax.rem(wide_row, pack) * nx
     pick_ref[...] = jnp.where((rank < live_of) & (goal == wide_lane), 1.0, 0.0).astype(jnp.float32)
 
+    owner = wide_lane // group
+    target = jnp.zeros_like(wide_row)
+    before = jnp.int32(0)
+    for i in range(nsub):
+        face = before - 1 + lax.rem(wide_lane // 8, 2) * counts_ref[i]
+        target = jnp.where(owner == i, face, target)
+        before = before + counts_ref[i]
+    at_face = (lax.rem(wide_row, nx) == target) & (wide_row // nx == lax.rem(wide_lane // yl_n, 2))
+    for y in range(yl_n):
+        ends_ref[y] = jnp.where(at_face & (lax.rem(wide_lane, yl_n) == y), 1.0, 0.0).astype(jnp.float32)
+
+    live_here = counts_ref[sub]
+    depth = perm_ref.shape[0] // 8
+
+    def plane(p):
+        return slice(8 * p, 8 * p + 8)
+
+    tall = lax.broadcasted_iota(jnp.int32, (8, LANES), 0)
+    long = lax.broadcasted_iota(jnp.int32, (8, LANES), 1)
+    for p in range(depth):
+        mine_perm = perm_ref[plane(p), :]
+        alive = jnp.where(p < live_here, 2.0, 0.0).astype(jnp.float32)
+        if p + 1 < depth:
+            other = perm_ref[plane(p + 1), :]
+            joined = jnp.where(p + 1 < live_here, 2.0, 0.0).astype(jnp.float32)
+            wall[0, plane(p), :] = joined * mine_perm * other / (mine_perm + other)
+        other = pltpu.roll(mine_perm, 7, 0)
+        wall[1, plane(p), :] = jnp.where(tall < 7, alive * mine_perm * other / (mine_perm + other), 0.0)
+        other = pltpu.roll(mine_perm, LANES - 1, 1)
+        wall[2, plane(p), :] = jnp.where(long < LANES - 1, alive * mine_perm * other / (mine_perm + other), 0.0)
+
     strip = lax.broadcasted_iota(jnp.int32, (zl, LANES), 1) // group
 
     def butterfly(items):
@@ -343,7 +375,7 @@
             for a in range(len(items)):
                 if a & d:
                     continue
-                first_half = (strip & d) == 0
+                first_half = (strip[0 : items[a].shape[0], :] & d) == 0
                 fresh[a] = jnp.where(first_half, items[a], pltpu.roll(items[a + d], group * d, 1))
                 fresh[a + d] = jnp.where(first_half, pltpu.roll(items[a], LANES - group * d, 1), items[a + d])
             items = fresh
@@ -566,9 +598,9 @@
                 if j + 1 < ITERS:
                     basis[j + 1, :, at] = value
                 if halo <= e < halo + zl:
-                    to = spot(e - halo, y)
-                    big[8 * (j + 1) : 8 * (j + 2), to] = value * diag_own[:, at]
-                    found[8 * j : 8 * (j + 1), to] = first * fields[0][:, at] + d1[:, at] + d2[:, at] + here[y]
+                    big[8 * (j + 1) : 8 * (j + 2), spot(e - halo, y)] = value * diag_own[:, at]
+                if halo - 1 <= e <= halo + zl:
+                    found[8 * j : 8 * (j + 1), spot(e - halo + 1, y)] = first * fields[0][:, at] + d1[:, at] + d2[:, at] + here[y]
 
     moves = first_swap
     for j in range(ITERS):
@@ -577,8 +609,6 @@
             for t in range(DEG):
                 advance(j, t, range(halo + t + 1, halo + zl - t - 1))
             reduce_begin(j, products(j))
-            if j:
-                reduce_middle(j - 1)
             for c in moves:
                 c.wait()
             if not j:
@@ -590,14 +620,23 @@
         else:
             for t in range(DEG):
                 advance(j, t, range(inset + t + 1, span - inset - t - 1))
+            for e in (halo - 1, halo + zl):
+                for y in range(yl_n):
+                    at = spot(e, y)
+                    found[8 * j : 8 * (j + 1), spot(e - halo + 1, y)] = (
+                        first * field_of(j)[:, at] + d1[:, at] + d2[:, at] + d3[:, at]
+                    )
         if (j + 1) % REACH == 0 and j + 1 < ITERS:
             moves = swap(j + 1, (j + 1) // REACH)
             for c in moves:
                 c.start()
         else:
             reduce_begin(j + 1, products(j + 1))
-            reduce_middle(j)
-    reduce_middle(ITERS)
+        if j == 2:
+            for r in range(3):
+                reduce_middle(r)
+    for r in range(3, ITERS + 1):
+        reduce_middle(r)
 
     rows = 8 * ITERS
     for r in range(ITERS + 1):
@@ -618,44 +657,148 @@
     solved = block_jordan(system, row)
     filled = jnp.concatenate([*solved, jnp.zeros((LANES - rows, LANES), jnp.float32)], axis=0)
     mix = filled.T[rows : rows + 8, :]
-    used = mix - pltpu.roll(mix * up_by, 8, 1) - pltpu.roll(mix * down_by, LANES - 8, 1)
     leaving = []
-
-    def deliver(f, k, peer):
-        return remote(
-            out_buf.at[peer, f * yl_n : (f + 1) * yl_n],
-            out_got.at[f * yl_n : (f + 1) * yl_n, rows_of(sub), :],
-            out_send.at[f, k], out_recv.at[f, sub], {"sub": peer},
+    half = zl // 2
+    capped = (mine == 0) | (mine == nsub - 1)
+
+    def part_of(f, q, peer):
+        if f < 2:
+            rows_at = pl.ds(pl.multiple_of(q * zl + f * half, 8), half)
+            return out_buf.at[peer, :, f * half : (f + 1) * half, :], out_got.at[:, rows_at, :]
+        if f == 2:
+            return rim_buf.at[peer, 0:zl], rim_got.at[q, 0:zl]
+        return rim_buf.at[peer, zl : zl + 8], rim_got.at[q, zl : zl + 8]
+
+    def send(f):
+        for d in range(nsub):
+            peer = lax.rem(sub + d, nsub)
+            src, dst = part_of(f, mine, peer)
+            c = remote(src, dst, out_send.at[f, d], out_recv.at[f, mine], {"sub": peer, "slab": home})
+            away = None
+            if d == 0:
+                away = home != slab
+            if f == 3:
+                away = capped if away is None else away & capped
+            if away is None:
+                c.start()
+            else:
+                pl.when(away)(c.start)
+            leaving.append((away, c))
+
+    def landed(f):
+        for q in range(nsub) if f < 3 else (0, nsub - 1):
+            src, dst = part_of(f, q, 0)
+            c = remote(src, dst, out_send.at[f, q], out_recv.at[f, q], dev(slab * nsub + q))
+            pl.when(slab * nsub + q != place)(c.wait_recv)
+
+    pieces = []
+    for f in range(2):
+        lo = (f * (half + 1)) * yl_n * LANES
+        hi = lo + (half + 1) * yl_n * LANES
+        piece = full(((1,), (0,)), mix[:, 0:rows], found[:, lo:hi])
+        pieces.append(piece)
+        for e in range(f * half, (f + 1) * half):
+            for y in range(yl_n):
+                k = (e + 1) * yl_n + y
+                at = k * LANES - lo
+                k = e * yl_n + y
+                if f == 0 or at + LANES <= hi - lo:
+                    out_ref[k * 8 : k * 8 + 8, :] = piece[:, at : at + LANES]
+        base = f * half * yl_n * 8
+        raw_ref[base : base + half * yl_n * 8, :] = full(
+            ((1,), (1,)), out_ref[base : base + half * yl_n * 8, :], pick_ref[...]
         )
-
+        for y in range(yl_n):
+            items = [raw_ref[pl.ds(base + y * 8 + i, half, stride=yl_n * 8), :] for i in range(nsub)]
+            for i, value in enumerate(butterfly(items)):
+                out_buf[i, y, f * half : (f + 1) * half, :] = value
+        send(f)
+
+    def sol_at(e, y):
+        k = (e + 1) * yl_n + y
+        f = k // ((half + 1) * yl_n)
+        at = (k - f * (half + 1) * yl_n) * LANES
+        return pieces[f][:, at : at + LANES]
+
+    @pl.when(home == slab)
+    def _():
+        out_got[:, rows_of(mine), :] = out_buf[sub]
+
+    for e in range(zl):
+        for y in range(yl_n):
+            at = spot(halo + e, y)
+            k = e * yl_n + y
+            value = out_ref[k * 8 : k * 8 + 8, :]
+            drop = value - pltpu.roll(value, LANES - 1, 1)
+            flux_ref[y, e * 8 : e * 8 + 8, :] = coef[0, :, at] * diag_own[:, at] * drop
+    faces = full(((1,), (0,)), flux_ref[0], ends_ref[0])
+    for y in range(1, yl_n):
+        faces = faces + full(((1,), (0,)), flux_ref[y], ends_ref[y])
+    for y in range(yl_n):
+        at = spot(halo, y)
+        flux_ref[0, y * 8 : y * 8 + 8, :] = coef[5, :, at] * diag_own[:, at] * (sol_at(-1, y) - sol_at(0, y))
+        at = spot(halo + zl - 1, y)
+        flux_ref[1, y * 8 : y * 8 + 8, :] = coef[4, :, at] * diag_own[:, at] * (sol_at(zl - 1, y) - sol_at(zl, y))
+    raw_ref[0 : zl * 8, :] = faces
     for f in range(2):
-        if f == 0:
-            mixture = full(((1,), (0,)), mix[:, 0:rows], found[...])
+        raw_ref[zl * 8 + f * yl_n * 8 : zl * 8 + (f + 1) * yl_n * 8, :] = full(
+            ((1,), (1,)), flux_ref[f, 0 : yl_n * 8, :], pick_ref[...]
+        )
+    for i, value in enumerate(butterfly([raw_ref[pl.ds(i, zl, stride=8), :] for i in range(nsub)])):
+        rim_buf[i, 0:zl, :] = value
+    send(2)
+    for i, value in enumerate(butterfly([raw_ref[pl.ds(zl * 8 + i, 8, stride=8), :] for i in range(nsub)])):
+        rim_buf[i, zl : zl + 8, :] = value
+    send(3)
+
+    @pl.when(home == slab)
+    def _():
+        rim_got[mine] = rim_buf[sub]
+
+    landed(0)
+    landed(1)
+    for y in range(yl_n):
+        out0_ref[pl.ds(y, LANES, stride=yl_n), :] = out_got[y].T
+    landed(2)
+    landed(3)
+    around = jnp.concatenate([rim_got[q, 0:zl, :] for q in range(nsub)], axis=0).T
+    caps = jnp.concatenate(
+        [rim_got[0, zl : zl + yl_n, :], rim_got[nsub - 1, zl + yl_n : zl + 8, :], jnp.zeros((LANES - 8, LANES), jnp.float32)],
+        axis=0,
+    ).T
+    for y in range(yl_n):
+        lower = jnp.broadcast_to(caps[:, y : y + 1], (LANES, LANES))
+        upper = jnp.broadcast_to(caps[:, yl_n + y : yl_n + y + 1], (LANES, LANES))
+        edge_ref[pl.ds(y, LANES, stride=yl_n), :] = jnp.where(
+            wide_lane == 0, lower, jnp.where(wide_lane == LANES - 1, -upper, 0.0)
+        )
+    for i in range(8):
+        def rows_at(p):
+            return slice((i * depth + p) * 8, (i * depth + p + 1) * 8)
+
+        carried = around[16 * i : 16 * i + 8, :]
+        beyond = around[16 * i + 8 : 16 * i + 16, :]
+        value = out0_ref[rows_at(0), :]
+        for p in range(depth):
+            alive = jnp.where(p < live_here, 1.0, 0.0).astype(jnp.float32)
+            final = jnp.where(p + 1 == live_here, 1.0, 0.0).astype(jnp.float32)
+            rest = alive * rhs_ref[rows_at(p), :] + edge_ref[rows_at(p), :] - accum_ref[plane(p), :] * value
+            rest = rest + carried - final * beyond
+            fy = wall[1, plane(p), :] * (value - pltpu.roll(value, 7, 0))
+            fz = wall[2, plane(p), :] * (value - pltpu.roll(value, LANES - 1, 1))
+            rest = rest - (fy - pltpu.roll(fy, 1, 0)) - (fz - pltpu.roll(fz, 1, 1))
+            if p + 1 < depth:
+                ahead = out0_ref[rows_at(p + 1), :]
+                carried = wall[0, plane(p), :] * (value - ahead)
+                rest = rest - carried
+                value = ahead
+            out1_ref[rows_at(p), :] = rest
+    for away, c in arrivals + leaving:
+        if away is None:
+            c.wait_send()
         else:
-            mixture = big[0:8, :] - full(((1,), (0,)), used[:, 0 : rows + 8], big[...])
-        for k in range(zl * yl_n):
-            out_ref[f, k * 8 : k * 8 + 8, :] = mixture[:, k * LANES : (k + 1) * LANES]
-        raw_ref[...] = full(((1,), (1,)), out_ref[f], pick_ref[...])
-        for y in range(yl_n):
-            items = [raw_ref[pl.ds(y * 8 + i, zl, stride=yl_n * 8), :] for i in range(nsub)]
-            for i, value in enumerate(butterfly(items)):
-                out_buf[i, f * yl_n + y] = value
-        for d in range(1, nsub):
-            c = deliver(f, d, lax.rem(sub + d, nsub))
-            c.start()
-            leaving.append(c)
-        out_got[f * yl_n : (f + 1) * yl_n, rows_of(sub), :] = out_buf[sub, f * yl_n : (f + 1) * yl_n]
-    for f, ref in enumerate((out0_ref, out1_ref)):
-        for d in range(1, nsub):
-            peer = lax.rem(sub + d, nsub)
-            remote(
-                out_buf.at[peer, f * yl_n : (f + 1) * yl_n],
-                out_got.at[f * yl_n : (f + 1) * yl_n, rows_of(peer), :],
-                out_send.at[f, d], out_recv.at[f, peer], {"sub": peer},
-            ).wait_recv()
-        for y in range(yl_n):
-            ref[pl.ds(y, LANES, stride=yl_n), :] = out_got[f * yl_n + y].T
-    for c in arrivals + leaving + sends:
+            pl.when(away)(c.wait_send)
+    for c in sends:
         c.wait_send()
 
 
@@ -687,12 +830,18 @@
             pltpu.SMEM((nsub,), jnp.int32),
             dma((4,)),
             pltpu.VMEM((LANES, LANES), f32),
+            pltpu.VMEM((yl, LANES, LANES), f32),
             pltpu.VMEM((zl * yl * s, LANES), f32),
-            pltpu.VMEM((2, zl * yl * s, LANES), f32),
+            pltpu.VMEM((zl * yl * s, LANES), f32),
+            pltpu.VMEM((yl, zl * s, LANES), f32),
             pltpu.VMEM((yl + 1, zs, LANES), f32),
             pltpu.VMEM((nsub, yl + 1, zl, LANES), f32),
-            pltpu.VMEM((nsub, 2 * yl, zl, LANES), f32),
-            pltpu.VMEM((2 * yl, zs, LANES), f32),
+            pltpu.VMEM((nsub, yl, zl, LANES), f32),
+            pltpu.VMEM((yl, zs, LANES), f32),
+            pltpu.VMEM((nsub, zl + 8, LANES), f32),
+            pltpu.VMEM((nsub, zl + 8, LANES), f32),
+            pltpu.VMEM((3, depth * cy, zs), f32),
+            pltpu.VMEM((s * depth * cy, zs), f32),
             pltpu.VMEM((8, (zl + 2 * pad) * LANES), f32),
             pltpu.VMEM((6, 8, wide), f32),
             pltpu.VMEM((8, wide), f32),
@@ -700,7 +849,7 @@
             pltpu.VMEM((8, wide), f32),
             pltpu.VMEM((ITERS, 8, wide), f32),
             pltpu.VMEM((8 * rounds, own), f32),
-            pltpu.VMEM((8 * ITERS, own), f32),
+            pltpu.VMEM((8 * ITERS, own + 2 * yl * LANES), f32),
             pltpu.VMEM((8, wide), f32),
             pltpu.VMEM((8, wide), f32),
             pltpu.VMEM((8, wide), f32),
@@ -712,8 +861,8 @@
             pltpu.VMEM((LANES, LANES), f32),
             dma((2, nsub)),
             dma((2, nsub)),
-            dma((2, nsub)),
-            dma((2, nsub)),
+            dma((4, nsub)),
+            dma((4, nsub)),
             dma((2,)),
             dma((2,)),
             dma((ITERS // REACH, 2)),
@@ -734,7 +883,7 @@
     nsub = lax.axis_size("sub")
     s, depth, cy, zs = rhs.shape
     nx = depth * nsub
-    fits = s == S == nsub == 8 and zs == LANES and zs // nsub % 8 == 0 and LANES % nx == 0 and zs % nsub == 0 and zs // nsub > DEG * REACH
+    fits = s == S == nsub == 8 and zs == LANES and depth == cy == 8 and zs // nsub % 8 == 0 and LANES % nx == 0 and zs % nsub == 0 and lax.axis_size("slab") % 2 == 0 and zs // nsub > DEG * REACH
     fits = fits and cy % max(LANES // nx, 1) == 0 and cy // max(LANES // nx, 1) == 4
     if fits:
         return fast_body(rhs, perm, accum, counts)

time: 59.4 us -> 54.3 us (0.914)
  Pallas kernels: 56.2 us -> 51.1 us
    pallas_call x1, Pallas kernels: 56.2 us -> 51.1 us  [fast_body(): pl.pallas_call(functools.partial(kernel, (nsub, nslab, zl, yl, pack, nx))...]
where the time goes in v3:
time: 54.3 us; the launch traced here: 54.2 us
  Pallas kernels  51.1 us (94%)
  local copies, waits for them, and re-layouts  2.42 us (4%)
  between operations  0.65 us (1%)
    pallas_call x1, Pallas kernels, fast_body(): pl.pallas_call(functools.partial(kernel, (nsub, nslab, zl, yl, pack, nx))...  51.1 us
    unnamed x4, local copies, waits for them, and re-layouts  2.42 us

profile of v3, /device:TPU:0, one launch (start us, length us, event | category | flops | bytes accessed | tf_op | source)
XLA Modules:
  0.0 54.2 jit_solution(7194846399098887239)
XLA Ops:
  0.6 51.1 %shard_map.59 = (f32[512,128]{1,0:T(8,128)}, f32[512,128]{1,0:T(8,128)}) custom-call(f32[512,128]{1,0:T(8,128)} %bitcast.5, f32[64,128]{1,0:T(8,128)} %bitcast.8, f32[64,128]{1,0:T(8,128)} %bitcast.9, s32[8]{0:T(128)} %counts_hbm.1), custom_call_target="tpu_custom_call" | custom-call | tf_op jit(solution)/shard_map/pallas_call | solution.py:821
  51.7 0.0 copy-start
  51.8 1.7 %copy.8 = f32[8,8,8,128]{3,2,1,0:T(8,128)} copy(f32[8,8,8,128]{3,2,1,0:T(8,128)} %bitcast.7) | data formatting | bytes 524288
  53.5 0.0 copy-done
  53.5 0.7 %copy.9 = f32[8,8,8,128]{3,2,1,0:T(8,128)} copy(f32[8,8,8,128]{3,2,1,0:T(8,128)S(1)} %bitcast.6) | data formatting | bytes 524288
Async XLA Ops:
  51.7 1.7 %copy-start = (f32[512,128]{1,0:T(8,128)S(1)}, f32[512,128]{1,0:T(8,128)}, u32[]{:S(2)}) copy-start(f32[512,128]{1,0:T(8,128)} %get-tuple-element.5) | copy-start | bytes 786436

commit v4 on v3

--- a/solution.py
+++ b/solution.py
@@ -295,10 +295,16 @@
         return pl.ds(pl.multiple_of(i * zl, 8), zl)
 
     halves = ((yl_n, 1), (0, yl_n))
+    flip = jnp.where(sub // 2 < nsub // 4, 1, 0)
+
+    def far_first(k):
+        return k // 2 + flip * (nsub // 2 - 1 - 2 * (k // 2))
+
     arrivals = []
     for k, (t, n) in enumerate(halves):
         for d in range(nsub):
-            q = lax.rem(mine + d, nsub)
+            deep = far_first(d)
+            q = 2 * (deep + lax.rem(slab, 2) * (nsub // 2 - 1 - 2 * deep)) + d % 2
             goal = slab * nsub + q
             c = remote(
                 in_buf.at[t : t + n, rows_of(q), :], in_got.at[sub, t : t + n],
@@ -402,6 +408,42 @@
     up.start()
     down.start()
 
+    along = lax.rem(lane, nx)
+
+    def fill(e, _):
+        def grab(t):
+            return ext[:, pl.ds(pl.multiple_of((e + 1 + t) * LANES, LANES), LANES)]
+
+        here, after, before = grab(0), grab(1), grab(-1)
+        swap_up = jnp.where(lane >= LANES - nx, 0.0, pltpu.roll(here, LANES - nx, 1))
+        swap_down = jnp.where(lane < nx, 0.0, pltpu.roll(here, nx, 1))
+        others = (
+            jnp.where(along == nx - 1, 0.0, pltpu.roll(here, LANES - 1, 1)),
+            jnp.where(along == 0, 0.0, pltpu.roll(here, 1, 1)),
+            jnp.where(row == yl_n - 1, pltpu.roll(swap_up, yl_n - 1, 0), pltpu.roll(here, 7, 0)),
+            jnp.where(row == 0, pltpu.roll(swap_down, 8 - (yl_n - 1), 0), pltpu.roll(here, 1, 0)),
+            after,
+            before,
+        )
+        diag = pltpu.roll(here, 8 - yl_n, 0)
+        weights = []
+        for q in others:
+            both = here * q
+            weight = jnp.where(both > 0.0, 2.0 * both / jnp.where(both > 0.0, here + q, 1.0), 0.0)
+            weights.append(weight)
+            diag = diag + weight
+        over = jnp.where(diag > 0.0, 1.0 / jnp.where(diag > 0.0, diag, 1.0), 0.0)
+        weights = [weight * over for weight in weights]
+        for y in range(yl_n):
+            at = pl.ds(pl.multiple_of((e * yl_n + y) * LANES, LANES), LANES)
+            for k, weight in enumerate(weights):
+                coef[k, :, at] = spread_rows(weight, y)
+            inv[:, at] = spread_rows(over, y)
+            diag_own[:, at] = spread_rows(diag, y)
+        return 0
+
+    lax.fori_loop(halo + 1, halo + zl - 1, fill, 0)
+
     arrived(1)
     for t in range(yl_n):
         for i, value in enumerate(butterfly([in_got[i, t] for i in range(nsub)])):
@@ -432,8 +474,8 @@
 
         def add(k, accs):
             accs = list(accs)
-            for h in range(2):
-                at = pl.ds(pl.multiple_of((2 * k + h) * LANES, LANES), LANES)
+            for h in range(4):
+                at = pl.ds(pl.multiple_of((4 * k + h) * LANES, LANES), LANES)
                 w = big[8 * j : 8 * j + 8, at]
                 turned = [w] + [pltpu.roll(w, n, 0) for n in range(1, 8)]
                 for b in range(blocks):
@@ -443,7 +485,7 @@
             return tuple(accs)
 
         zero = jnp.zeros((8, LANES), jnp.float32)
-        accs = lax.fori_loop(0, zl * yl_n // 2, add, (zero,) * (8 * blocks))
+        accs = lax.fori_loop(0, zl * yl_n // 4, add, (zero,) * (8 * blocks))
         out = zero
         for b in range(blocks):
             for n in range(8):
@@ -497,49 +539,8 @@
         ext[:, a : a + LANES] = ext[:, a : a + LANES] * low
         b = (pad + zl + k) * LANES
         ext[:, b : b + LANES] = ext[:, b : b + LANES] * high
-    along = lax.rem(lane, nx)
-
-    def fill(e, _):
-        def grab(t):
-            return ext[:, pl.ds(pl.multiple_of((e + 1 + t) * LANES, LANES), LANES)]
-
-        here, after, before = grab(0), grab(1), grab(-1)
-        swap_up = pltpu.roll(here, LANES - nx, 1)
-        swap_down = pltpu.roll(here, nx, 1)
-        x_up = jnp.where(along == nx - 1, 0.0, pltpu.roll(here, LANES - 1, 1))
-        x_down = jnp.where(along == 0, 0.0, pltpu.roll(here, 1, 1))
-        swap_up = jnp.where(lane >= LANES - nx, 0.0, swap_up)
-        swap_down = jnp.where(lane < nx, 0.0, swap_down)
-
-        def line(value, y):
-            return jnp.broadcast_to(value[y : y + 1, :], (8, LANES))
-
-        for y in range(yl_n):
-            p = line(here, y)
-            others = (
-                line(x_up, y),
-                line(x_down, y),
-                line(here, y + 1) if y + 1 < yl_n else line(swap_up, 0),
-                line(here, y - 1) if y > 0 else line(swap_down, yl_n - 1),
-                line(after, y),
-                line(before, y),
-            )
-            at = pl.ds(pl.multiple_of((e * yl_n + y) * LANES, LANES), LANES)
-            diag = line(here, yl_n + y)
-            weights = []
-            for q in others:
-                both = p * q
-                weight = jnp.where(both > 0.0, 2.0 * both / jnp.where(both > 0.0, p + q, 1.0), 0.0)
-                weights.append(weight)
-                diag = diag + weight
-            over = jnp.where(diag > 0.0, 1.0 / jnp.where(diag > 0.0, diag, 1.0), 0.0)
-            for k, weight in enumerate(weights):
-                coef[k, :, at] = weight * over
-            inv[:, at] = over
-            diag_own[:, at] = diag
-        return 0
-
-    lax.fori_loop(0, span, fill, 0)
+    lax.fori_loop(0, halo + 1, fill, 0)
+    lax.fori_loop(halo + zl - 1, span, fill, 0)
 
     def scale(lo, hi):
         for k in range(lo * yl_n, hi * yl_n):
@@ -671,18 +672,13 @@
 
     def send(f):
         for d in range(nsub):
-            peer = lax.rem(sub + d, nsub)
+            peer = 2 * far_first(d) + d % 2
             src, dst = part_of(f, mine, peer)
             c = remote(src, dst, out_send.at[f, d], out_recv.at[f, mine], {"sub": peer, "slab": home})
-            away = None
-            if d == 0:
-                away = home != slab
+            away = (home != slab) | (peer != sub)
             if f == 3:
-                away = capped if away is None else away & capped
-            if away is None:
-                c.start()
-            else:
-                pl.when(away)(c.start)
+                away = away & capped
+            pl.when(away)(c.start)
             leaving.append((away, c))
 
     def landed(f):
@@ -794,10 +790,7 @@
                 value = ahead
             out1_ref[rows_at(p), :] = rest
     for away, c in arrivals + leaving:
-        if away is None:
-            c.wait_send()
-        else:
-            pl.when(away)(c.wait_send)
+        pl.when(away)(c.wait_send)
     for c in sends:
         c.wait_send()
 

time: 54.3 us -> 52.6 us (0.969)
  Pallas kernels: 51.1 us -> 49.4 us
    pallas_call x1, Pallas kernels: 51.1 us -> 49.4 us  [fast_body(): pl.pallas_call(functools.partial(kernel, (nsub, nslab, zl, yl, pack, nx))...]
where the time goes in v4:
time: 52.6 us; the launch traced here: 52.4 us
  Pallas kernels  49.4 us (94%)
  local copies, waits for them, and re-layouts  2.42 us (5%)
  between operations  0.65 us (1%)
    pallas_call x1, Pallas kernels, fast_body(): pl.pallas_call(functools.partial(kernel, (nsub, nslab, zl, yl, pack, nx))...  49.4 us
    unnamed x4, local copies, waits for them, and re-layouts  2.42 us

profile of v4, /device:TPU:0, one launch (start us, length us, event | category | flops | bytes accessed | tf_op | source)
XLA Modules:
  0.0 52.4 jit_solution(14751529023574189533)
XLA Ops:
  0.6 49.4 %shard_map.59 = (f32[512,128]{1,0:T(8,128)}, f32[512,128]{1,0:T(8,128)}) custom-call(f32[512,128]{1,0:T(8,128)} %bitcast.5, f32[64,128]{1,0:T(8,128)} %bitcast.8, f32[64,128]{1,0:T(8,128)} %bitcast.9, s32[8]{0:T(128)} %counts_hbm.1), custom_call_target="tpu_custom_call" | custom-call | tf_op jit(solution)/shard_map/pallas_call | solution.py:814
  50.0 0.0 copy-start
  50.0 1.7 %copy.8 = f32[8,8,8,128]{3,2,1,0:T(8,128)} copy(f32[8,8,8,128]{3,2,1,0:T(8,128)} %bitcast.7) | data formatting | bytes 524288
  51.7 0.0 copy-done
  51.7 0.7 %copy.9 = f32[8,8,8,128]{3,2,1,0:T(8,128)} copy(f32[8,8,8,128]{3,2,1,0:T(8,128)S(1)} %bitcast.6) | data formatting | bytes 524288
Async XLA Ops:
  50.0 1.7 %copy-start = (f32[512,128]{1,0:T(8,128)S(1)}, f32[512,128]{1,0:T(8,128)}, u32[]{:S(2)}) copy-start(f32[512,128]{1,0:T(8,128)} %get-tuple-element.5) | copy-start | bytes 786436
